TPU v7x, 256 devices: a whole 4x4x8 slice. The times are simulated.
256 devices in a mesh: dp: 8 (over y, x_lo), seq: 32 (over z, x_hi, core).
Axes of the slice: x: 4 (x_hi: 2, x_lo: 2; x = x_hi * 2 + x_lo), y: 4, z: 8, core: 2. Of those that a mesh axis runs over, the one named last changes fastest.
Arguments:
- tokens: bfloat16 [8, 16384, 2560], P('dp', 'seq'), may hold values from -6 to 6
- w_x: bfloat16 [2560, 3072], P('seq'), may hold values from -0.125 to 0.125
- w_bc: bfloat16 [2560, 256], P('seq'), may hold values from -0.125 to 0.125
- w_dt: bfloat16 [2560, 48], P('seq'), may hold values from -0.125 to 0.125
- dt_bias: float32 [48], replicated, may hold values from -1 to 0.5
- decay_rate: float32 [48], replicated, may hold values from 2.4414063e-05 to 0.12
- gain: float32 [3072], replicated, may hold values from 0.5 to 1.5
- cotangent: bfloat16 [8, 16384, 3072], P('dp', 'seq'), may hold values from -0.005859375 to 0.005859375
- counts: int32 [32], replicated, may hold values from 1 to 2, 48 in all
Outputs:
- ssm_output: bfloat16 [8, 16384, 3072], P('dp', 'seq')
- grad_c: float32 [2560, 128], P('seq')
Inputs may be any that keep to these rules, and one draw needn't show every extreme that they name: counts add up to 48 and one of them equals 2.
All inputs are finite; a program needn't handle non-finite values.
Results may differ from a plain program's by a relative error of at most 0.02.
Values may be sent and summed in bfloat16 or wider, within the bound.
A program may use at most 128 MiB of HBM per device.

v0:
```python
import jax
import jax.numpy as jnp
from jax import lax
from jax.sharding import Mesh
from jax.sharding import PartitionSpec as P

L = 256
SEQ = ("seq_0", "seq_1", "seq_2")


norm_floor = 1.0


def in_one_piece(arrays, axis, dim, along):
    both = jnp.concatenate(arrays, axis=along)
    whole, at, done = (lax.all_gather(both, axis, axis=dim, tiled=True), 0, [])
    for a in arrays:
        done.append(lax.slice_in_dim(whole, at, at + a.shape[along], axis=along))
        at += a.shape[along]
    return tuple(done)


def nothing_yet(shard, identity):
    return jax.tree.map(
        lambda a, e: jnp.broadcast_to(jnp.asarray(e, a.dtype), a.shape), shard, identity
    )


def entering(shard, axes, combine, identity):
    before = start = nothing_yet(shard, identity)
    subtotal = shard
    for axis in reversed(axes):
        peers, place = (lax.axis_size(axis), lax.axis_index(axis))
        pieces = jax.tree.map(
            lambda part, kind: lax.all_gather(part.astype(kind), axis),
            subtotal,
            (jnp.bfloat16, jnp.bfloat16),
        )
        inside, subtotal = (start, start)
        for k in range(peers):
            passed = k < place
            subtotal = combine(
                subtotal, jax.tree.map(lambda part, own: part[k].astype(own.dtype), pieces, shard)
            )
            inside = jax.tree.map(lambda new, old: jnp.where(passed, new, old), subtotal, inside)
        before = combine(inside, before)
    return before


def cut_along(shard, dim, peers):
    shape = shard.shape
    blocks = shard.reshape(*shape[:dim], peers, shape[dim] // peers, *shape[dim + 1 :])
    return jnp.moveaxis(blocks, dim, 0)


def sum_at_owner(shard, axis, dim):
    blocks = cut_along(shard, dim, lax.axis_size(axis))
    arrived = lax.all_to_all(blocks, axis, split_axis=0, concat_axis=0, tiled=True)
    return arrived.astype(jnp.float32).sum(axis=0)


def copy_for_each(shard, axis):
    peers = lax.axis_size(axis)
    return lax.all_to_all(
        jnp.broadcast_to(shard[None], (peers, *shard.shape)), axis, 0, 0, tiled=True
    )


def taken_together(shard, axis):
    return copy_for_each(shard, axis).astype(jnp.float32).sum(axis=0)


def scale_state(state, decay):
    return (state.reshape(decay.shape[0], -1) * decay[:, None]).reshape(state.shape)


def combine_states(earlier, later):
    return (earlier[0] * later[0], scale_state(earlier[1], later[0]) + later[1])


def decay_weights(cumulative, dt_rows):
    length = cumulative.shape[0]
    causal = jnp.arange(length)[:, None] >= jnp.arange(length)[None, :]
    gap_log = cumulative.T[:, :, None] - cumulative.T[:, None, :]
    gap_log = jnp.where(causal[None, :, :], gap_log, -jnp.inf)
    return jnp.exp(gap_log) * dt_rows.T[:, None, :]


def stretch_state(inner, b_proj, dt_rows, a_neg):
    length = inner.shape[0]
    head_count = a_neg.shape[0]
    cumulative = jnp.cumsum(dt_rows * a_neg[None, :], axis=0)
    to_end = jnp.exp(cumulative[-1][None, :] - cumulative) * dt_rows
    scaled = (
        (inner.reshape(length, head_count, -1) * to_end[:, :, None])
        .reshape(length, -1)
        .astype(jnp.bfloat16)
    )
    state_add = jnp.dot(scaled.T, b_proj, preferred_element_type=jnp.float32)
    return (jnp.exp(cumulative[-1]), state_add)


def stretch_outputs(inner, b_proj, c_proj, dt_rows, a_neg, state_in, gain, cot_rows, slot_used):
    length = inner.shape[0]
    head_count = a_neg.shape[0]
    head_size = inner.shape[1] // head_count
    cumulative = jnp.cumsum(dt_rows * a_neg[None, :], axis=0)
    weights = decay_weights(cumulative, dt_rows)
    gram_mat = jnp.dot(c_proj, b_proj.T, preferred_element_type=jnp.float32)
    mixing = (gram_mat[None, :, :] * weights).astype(jnp.bfloat16)
    inner_heads = inner.reshape(length, head_count, head_size)
    y_intra = jnp.einsum("hts,shp->thp", mixing, inner_heads, preferred_element_type=jnp.float32)
    state_low = state_in.astype(jnp.bfloat16)
    growth = jnp.exp(cumulative)[:, :, None]
    y_inter = (
        jnp.dot(c_proj, state_low.T, preferred_element_type=jnp.float32).reshape(
            length, head_count, head_size
        )
        * growth
    )
    full = y_intra + y_inter
    radius = jnp.sqrt(jnp.mean(full * full, axis=2, keepdims=True) + norm_floor)
    gain_heads = gain.reshape(head_count, head_size)
    output = (full / radius * gain_heads * slot_used).reshape(length, -1).astype(jnp.bfloat16)
    grad_out = cot_rows.reshape(length, head_count, head_size) * gain_heads
    grad_full = (
        grad_out / radius
        - full * jnp.sum(grad_out * full, axis=2, keepdims=True) / (head_size * radius**3)
    ) * slot_used
    grad_low = grad_full.astype(jnp.bfloat16)
    intersect = jnp.einsum(
        "thp,shp->hts", grad_low, inner_heads, preferred_element_type=jnp.float32
    )
    combined = jnp.sum(intersect * weights, axis=0).astype(jnp.bfloat16)
    grad_intra = jnp.dot(combined, b_proj, preferred_element_type=jnp.float32)
    scaled_grad = (grad_full * growth).reshape(length, -1).astype(jnp.bfloat16)
    grad_inter = jnp.dot(scaled_grad, state_low, preferred_element_type=jnp.float32)
    return (output, (grad_intra + grad_inter).astype(jnp.bfloat16))


def body(tokens, w_x, w_bc, w_dt, dt_bias, decay_rate, gain, cotangent, counts):
    seq_tokens = tokens[0]
    cot_rows = cotangent[0]
    row_total = seq_tokens.shape[0]
    slot_count = row_total // L
    state_size = w_bc.shape[1] // 2
    head_count = decay_rate.shape[0]
    group_index = lax.axis_index(SEQ)
    filled = jnp.sum(jnp.where(jnp.arange(counts.shape[0]) == group_index, counts, 0))
    slot_used = (jnp.arange(slot_count) < filled).astype(jnp.float32)
    pieces = in_one_piece((w_x, w_bc, w_dt), SEQ, 0, 1)
    columns = seq_tokens
    inner_sum, bc_raw, dt_raw = tuple(
        (jnp.dot(columns, block_rows, preferred_element_type=jnp.float32) for block_rows in pieces)
    )
    inner = inner_sum.astype(jnp.bfloat16)
    b_proj = bc_raw[:, :state_size].astype(jnp.bfloat16)
    c_proj = bc_raw[:, state_size:].astype(jnp.bfloat16)
    a_neg = -decay_rate
    dt_blocks = (
        jax.nn.softplus(dt_raw + dt_bias).reshape(slot_count, L, head_count)
        * slot_used[:, None, None]
    )
    inner_blocks = inner.reshape(slot_count, L, -1)
    b_blocks = b_proj.reshape(slot_count, L, -1)
    c_blocks = c_proj.reshape(slot_count, L, -1)
    cot_blocks = cot_rows.reshape(slot_count, L, -1)
    decays, additions = lax.map(
        lambda stretch_data: stretch_state(
            stretch_data[0], stretch_data[1], stretch_data[2], a_neg
        ),
        (inner_blocks, b_blocks, dt_blocks),
    )

    def advance(running, stretch_data):
        return (combine_states(running, stretch_data), running)

    starting_state = (
        jnp.ones((head_count,), jnp.float32),
        jnp.zeros(additions.shape[1:], jnp.float32),
    )
    (dev_decay, dev_state), (prior_decay, prior_state) = lax.scan(
        advance, starting_state, (decays, additions)
    )
    unused_decay, state_before = entering(
        (dev_decay, dev_state), SEQ, combine_states, starting_state
    )
    state_in = (state_before.reshape(head_count, -1)[None, :, :] * prior_decay[:, :, None]).reshape(
        prior_state.shape
    ) + prior_state
    outputs, grad_blocks = lax.map(
        lambda stretch_data: stretch_outputs(
            stretch_data[0],
            stretch_data[1],
            stretch_data[2],
            stretch_data[3],
            a_neg,
            stretch_data[4],
            gain,
            stretch_data[5],
            stretch_data[6],
        ),
        (inner_blocks, b_blocks, c_blocks, dt_blocks, state_in, cot_blocks, slot_used),
    )
    ssm_output = outputs.reshape(row_total, -1)
    grad_c_rows = grad_blocks.reshape(row_total, -1)
    columns = seq_tokens
    partial_rows = sum_at_owner(
        jnp.dot(columns.T, grad_c_rows, preferred_element_type=jnp.float32).astype(jnp.bfloat16),
        SEQ,
        0,
    )
    gradient = taken_together(partial_rows.astype(jnp.bfloat16), "dp").astype(jnp.float32)
    return (ssm_output[None], gradient)


def solution(mesh):
    finer = Mesh(mesh.devices.reshape(mesh.shape["dp"], 8, 2, 2), ("dp", "seq_0", "seq_1", "seq_2"))
    return jax.shard_map(
        body,
        mesh=finer,
        in_specs=(
            P("dp", SEQ, None),
            P(SEQ, None),
            P(SEQ, None),
            P(SEQ, None),
            P(),
            P(),
            P(),
            P("dp", SEQ, None),
            P(),
        ),
        out_specs=(P("dp", SEQ, None), P(SEQ, None)),
        check_vma=False,
    )
```

profile of v0, /device:TPU:4, one launch (start us, length us, event | category | flops | bytes accessed | tf_op | source)
XLA Modules:
  0.0 469.2 jit_solution(2447213147966971104)
XLA Ops:
  11.5 142.0 %all-gather.9.cloned.1.call-done = bf16[2560,3376]{1,0:T(8,128)(2,1)} async-done(((bf16[80,3376]{1,0:T(8,128)(2,1)}), bf16[2560,3376]{1,0:T(8,128)(2,1)}) %all-gather.9.cloned.1.call-update) | async-done | bytes 17285136 | tf_op jit(solution)/shard_map/all_gather | solution.py:16
  156.0 12.8 %fusion.51 = bf16[3072,512]{0,1:T(8,128)(2,1)} fusion(bf16[2560,3376]{1,0:T(8,128)(2,1)} %all-gather.9.cloned.1.call-done, bf16[1,512,2560]{2,1,0:T(8,128)(2,1)S(1)} %copy-done), kind=kOutput, calls=%fused_computation.86 | convolution fusion | flops 8054636544 | bytes 21495808 | tf_op jit(solution)/shard_map/dot_general | solution.py:154
  168.8 4.7 copy.78
  177.5 14.0 %while.41 = (s32[]{:T(128)}, f32[2,48]{1,0:T(2,128)S(1)}, f32[2,3072,128]{2,1,0:T(8,128)}, f32[2,256,48]{1,2,0:T(8,128)S(1)}, f32[48]{0:T(128)S(1)}, /*index=5*/...) while((s32[]{:T(128)}, f32[2,48]{1,0:T(2,128)S(1)}, ...), condition=%wide.region_4.5_spmd, body=%wide.region_1.4_spmd.sunk | while | flops 205308048 | bytes 35166580 | solution.py:168
  193.4 10.3 %while.43 = (s32[]{:T(128)}, f32[48]{0:T(128)S(1)}, f32[3072,128]{1,0:T(8,128)}, f32[2,48]{1,0:T(2,128)S(1)}, f32[2,3072,128]{2,1,0:T(8,128)}, /*index=5*/f32[2,...) while((s32[]{:T(128)}, f32[48]{0:T(128)S(1)}, f32[3072,128]{1,0:T(8,128)}, ...), condition=%wide.region_6.7_spmd.clone, body=%wide.region_5.6_spmd.clone.sunk | while | flops 1572963 | bytes 20498576 | solution.py:182
  197.9 2.8 bitcast_dynamic-update-slice_fusion.2
  200.7 3.0 bitcast_add_fusion.3
  210.3 5.7 %all-gather.2 = bf16[2,1,48]{2,1,0:T(2,128)(2,1)S(1)} all-gather(bf16[1,1,48]{2,1,0:T(2,128)(2,1)S(1)} %convert_bitcast_fusion.4), channel_id=1, replica_groups=mesh['dp'=8,'seq_0'=8,'seq_1'=2,'seq_2'=2] {'seq_1'}, dimensions={0}, use_global_device_ids=true | all-gather | bytes 288 | tf_op jit(solution)/shard_map/all_gather | solution.py:35
  216.5 4.2 all-gather.15.cloned.1.call-done
  220.7 3.5 fusion.72
  224.5 32.2 %all-gather.11.cloned.1.call-done = bf16[2,3072,128]{2,1,0:T(8,128)(2,1)} async-done(((bf16[1,3072,128]{2,1,0:T(8,128)(2,1)}), bf16[2,3072,128]{2,1,0:T(8,128)(2,1)}) %all-gather.11.cloned.1.call-update) | async-done | bytes 1572880 | tf_op jit(solution)/shard_map/all_gather | solution.py:35
  256.8 3.5 fusion.63
  273.3 2.7 mul.589
  276.0 17.5 %all-gather.3 = bf16[8,1,48]{2,1,0:T(2,128)(2,1)S(1)} all-gather(bf16[1,1,48]{2,1,0:T(2,128)(2,1)S(1)} %multiply_convert_fusion.6), channel_id=1, replica_groups=mesh['dp'=8,'seq_0'=8,'seq_1'=2,'seq_2'=2] {'seq_0'}, dimensions={0}, use_global_device_ids=true | all-gather | bytes 864 | tf_op jit(solution)/shard_map/all_gather | solution.py:35
  298.9 2.6 mul.557
  310.6 2.6 mul.566
  332.9 4.1 all-gather.13.cloned.1.call-done
  337.0 11.4 %fusion.68 = f32[3072,128]{1,0:T(8,128)S(1)} fusion(f32[3072,128]{1,0:T(8,128)} %mul.586, f32[3072,128]{1,0:T(8,128)} %mul.578, f32[3072,128]{1,0:T(8,128)} %mul.591, f32[3072,128]{1,0:T(8,128)} %mul.589, f32[3072,128]{1,0:T(8,128)} %mul.583, f32[3072,128]{1,0:T(8,128)} %mul.581, f32[3072,128]{1,0:T(8,128)} %mul.572, f32[3072,128]{1,0:T(8,128)} %mul.569, ...), kind=kLoop, calls=%fused_computation.111 | loop fusion | flops 19267584 | bytes 33030156 | tf_op jit(solution)/shard_map/add | solution.py:78
  350.3 70.5 %while.42 = (s32[]{:T(128)}, bf16[2,256,3072]{2,1,0:T(8,128)(2,1)}, bf16[2,256,128]{2,1,0:T(8,128)(2,1)S(1)}, bf16[2,256,3072]{1,2,0:T(8,128)(2,1)}, bf16[2,256,...) while((s32[]{:T(128)}, bf16[2,256,3072]{2,1,0:T(8,128)(2,1)}, ...), condition=%wide.region_13.14_spmd, body=%wide.region_7.13_spmd.sunk | while | flops 1291211008 | bytes 81402336 | solution.py:191
  354.6 5.9 %multiply_reduce_fusion.4 = (f32[256,48]{0,1:T(8,128)S(1)}, f32[256,48,64]{0,2,1:T(8,128)}) fusion(f32[256,48,64]{0,2,1:T(8,128)S(1)} %fusion.162, f32[256,48]{0,1:T(8,128)S(1)} %exponential_bitcast_fusion.2, bf16[256,48,64]{0,2,1:T(8,128)(2,1)S(1)} %bitcast.385, f32[48,256]{1,0:T(8,128)S(1)} %dynamic-slice_bitcast_fusion.2, ...), kind=kOutput, calls=%fused_computation.43.clone.1 | convolution fusion | flops 421515264 | bytes 8388608 | tf_op jit(solution)/shard_map/while/body/eval_jaxpr/hts,shp->thp/dot_general | solution.py:112
  361.2 3.7 multiply_convert_fusion.9
  364.9 2.6 copy.123
  367.5 3.7 constant_dynamic-slice_fusion.9
  373.9 6.2 %multiply_convert_fusion.10 = (bf16[256,48,64]{0,2,1:T(8,128)(2,1)S(1)}, bf16[256,48,64]{0,2,1:T(8,128)(2,1)S(1)}) fusion(f32[256,48]{0,1:T(8,128)S(1)} %exponential_bitcast_fusion.2, f32[]{:T(128)} %bitcast.373, f32[256,48]{0,1:T(8,128)S(1)} %get-tuple-element.549, f32[256,48,64]{0,2,1:T(8,128)} %get-tuple-element.545, ...), kind=kOutput, calls=%fused_computation.41.clone.1 | output fusion | flops 10235967 | bytes 8024068 | tf_op jit(solution)/shard_map/while/body/eval_jaxpr/mul | solution.py:128
  380.1 4.6 multiply_reduce_fusion.5
  389.8 5.9 %multiply_reduce_fusion.4 = (f32[256,48]{0,1:T(8,128)S(1)}, f32[256,48,64]{0,2,1:T(8,128)}) fusion(f32[256,48,64]{0,2,1:T(8,128)S(1)} %fusion.162, f32[256,48]{0,1:T(8,128)S(1)} %exponential_bitcast_fusion.2, bf16[256,48,64]{0,2,1:T(8,128)(2,1)S(1)} %bitcast.385, f32[48,256]{1,0:T(8,128)S(1)} %dynamic-slice_bitcast_fusion.2, ...), kind=kOutput, calls=%fused_computation.43.clone.1 | convolution fusion | flops 421515264 | bytes 8388608 | tf_op jit(solution)/shard_map/while/body/eval_jaxpr/hts,shp->thp/dot_general | solution.py:112
  396.5 3.7 multiply_convert_fusion.9
  402.8 3.7 constant_dynamic-slice_fusion.9
  409.1 6.2 %multiply_convert_fusion.10 = (bf16[256,48,64]{0,2,1:T(8,128)(2,1)S(1)}, bf16[256,48,64]{0,2,1:T(8,128)(2,1)S(1)}) fusion(f32[256,48]{0,1:T(8,128)S(1)} %exponential_bitcast_fusion.2, f32[]{:T(128)} %bitcast.373, f32[256,48]{0,1:T(8,128)S(1)} %get-tuple-element.549, f32[256,48,64]{0,2,1:T(8,128)} %get-tuple-element.545, ...), kind=kOutput, calls=%fused_computation.41.clone.1 | output fusion | flops 10235967 | bytes 8024068 | tf_op jit(solution)/shard_map/while/body/eval_jaxpr/mul | solution.py:128
  415.4 4.6 multiply_reduce_fusion.5
  422.4 27.9 %all_to_all.10 = bf16[32,80,128]{2,1,0:T(8,128)(2,1)S(1)} all-to-all(bf16[32,80,128]{2,1,0:T(8,128)(2,1)} %bitcast.391), channel_id=1, replica_groups=mesh['dp'=8,'seq_0'=8,'seq_1'=2,'seq_2'=2] {'seq_0','seq_1','seq_2'}, dimensions={0} | all-to-all | bytes 1310720 | tf_op jit(solution)/shard_map/all_to_all | solution.py:58
  450.5 11.5 %all_to_all.11 = bf16[8,80,128]{2,1,0:T(8,128)(2,1)S(1)} all-to-all(bf16[8,80,128]{2,1,0:T(8,128)(2,1)S(1)} %broadcast_in_dim.50), channel_id=1, replica_groups=mesh['dp'=8,'seq_0'=8,'seq_1'=2,'seq_2'=2] {'dp'}, dimensions={0} | all-to-all | bytes 327680 | tf_op jit(solution)/shard_map/all_to_all | solution.py:64
  (198 shorter events, 108.3 us)
Async XLA Ops:
  7.2 146.4 %copy-start = (bf16[1,512,2560]{2,1,0:T(8,128)(2,1)S(1)}, bf16[1,512,2560]{2,1,0:T(8,128)(2,1)}, u32[]{:S(2)}) copy-start(bf16[1,512,2560]{2,1,0:T(8,128)(2,1)} %param.15) | copy-start | bytes 7864324
  7.2 3.0 copy-start.11
  7.2 3.1 copy-start.12
  7.2 146.4 %all-gather.9.cloned.1.call-start = ((), (), s32[]{:S(2)}) async-start(), calls=%async_computation.2 | async-start | bytes 18247680 | tf_op jit(solution)/shard_map/all_gather | solution.py:16
  10.1 210.5 %all-gather.15.cloned.1.call-start = ((), (), s32[]{:S(2)}) async-start(), calls=%async_computation.5 | async-start | bytes 2359296 | tf_op jit(solution)/shard_map/all_gather | solution.py:35
  168.8 4.7 copy-start.10
  180.3 1.9 copy-start.5
  182.7 1.7 copy-start.6
  187.3 1.9 copy-start.5
  189.7 1.7 copy-start.6
  193.6 2.5 copy-start.7
  197.9 2.8 copy-start.7
  203.8 2.5 copy-start.13
  206.2 50.6 %all-gather.11.cloned.1.call-start = ((), (), s32[]{:S(2)}) async-start(), calls=%async_computation.3 | async-start | bytes 2359296 | tf_op jit(solution)/shard_map/all_gather | solution.py:35
  224.2 112.8 %all-gather.13.cloned.1.call-start = ((), (), s32[]{:S(2)}) async-start(), calls=%async_computation.4 | async-start | bytes 7077888 | tf_op jit(solution)/shard_map/all_gather | solution.py:35
  337.0 11.4 %copy-start.8 = (f32[2,3072,128]{2,1,0:T(8,128)S(1)}, f32[2,3072,128]{2,1,0:T(8,128)}, u32[]{:S(2)}) copy-start(f32[2,3072,128]{2,1,0:T(8,128)} %get-tuple-element.148) | copy-start | bytes 9437188
  348.4 1.9 copy-start.9
  352.5 1.9 copy-start.1
  354.5 5.9 %copy-start.3 = (bf16[1,256,3072]{1,2,0:T(8,128)(2,1)}, bf16[1,256,3072]{1,2,0:T(8,128)(2,1)S(1)}, u32[]{:S(2)}) copy-start(bf16[1,256,3072]{1,2,0:T(8,128)(2,1)S(1)} %constant_dynamic-slice_fusion.8) | copy-start | bytes 4718596 | tf_op jit(solution)/shard_map/while
  373.9 6.3 %copy-start.4 = (bf16[1,256,3072]{1,2,0:T(8,128)(2,1)S(1)}, bf16[1,256,3072]{1,2,0:T(8,128)(2,1)}, u32[]{:S(2)}) copy-start(bf16[1,256,3072]{1,2,0:T(8,128)(2,1)} %copy-done.3) | copy-start | bytes 4718596 | tf_op jit(solution)/shard_map/while
  380.1 4.8 %copy-start.2 = (bf16[2,3072,128]{2,1,0:T(8,128)(2,1)S(1)}, bf16[2,3072,128]{2,1,0:T(8,128)(2,1)}, u32[]{:S(2)}) copy-start(bf16[2,3072,128]{2,1,0:T(8,128)(2,1)} %get-tuple-element.656) | copy-start | bytes 4718596 | tf_op jit(solution)/shard_map/while
  387.8 1.9 copy-start.1
  389.8 5.9 %copy-start.3 = (bf16[1,256,3072]{1,2,0:T(8,128)(2,1)}, bf16[1,256,3072]{1,2,0:T(8,128)(2,1)S(1)}, u32[]{:S(2)}) copy-start(bf16[1,256,3072]{1,2,0:T(8,128)(2,1)S(1)} %constant_dynamic-slice_fusion.8) | copy-start | bytes 4718596 | tf_op jit(solution)/shard_map/while
  409.1 6.3 %copy-start.4 = (bf16[1,256,3072]{1,2,0:T(8,128)(2,1)S(1)}, bf16[1,256,3072]{1,2,0:T(8,128)(2,1)}, u32[]{:S(2)}) copy-start(bf16[1,256,3072]{1,2,0:T(8,128)(2,1)} %copy-done.3) | copy-start | bytes 4718596 | tf_op jit(solution)/shard_map/while
  415.4 4.8 %copy-start.2 = (bf16[2,3072,128]{2,1,0:T(8,128)(2,1)S(1)}, bf16[2,3072,128]{2,1,0:T(8,128)(2,1)}, u32[]{:S(2)}) copy-start(bf16[2,3072,128]{2,1,0:T(8,128)(2,1)} %get-tuple-element.656) | copy-start | bytes 4718596 | tf_op jit(solution)/shard_map/while
Sparse Core Ops, SparseCore 0:
  11.3 142.2 all-gather.8
  206.3 14.3 all-gather.14
  224.3 32.4 all-gather.10
  260.4 76.5 all-gather.12
where the time goes:
time: 471 us; the launch traced here: 469 us
  waiting for transfers between devices  183 us (39%)
  local copies, waits for them, and re-layouts  103 us (22%)
  blocking collectives  65.1 us (14%)
  other arithmetic  60.1 us (13%)
  matrix products  42.9 us (9%)
  between operations  14.7 us (3%)
    all_gather x1, waiting for transfers between devices, in_one_piece(): whole, at, done = (lax.all_gather(both, axis, axis=dim, tiled=True), 0, [])  142 us
    mul x40, local copies, waits for them, and re-layouts, scale_state(): state.reshape(decay.shape[0], -1) * decay[:, None]  55.6 us
    all_gather x3, waiting for transfers between devices, entering(): lax.all_gather(part.astype(kind), axis)  40.5 us
    all_to_all x1, blocking collectives, sum_at_owner(): lax.all_to_all(blocks, axis, split_axis=0, concat_axis=0, tiled=True)  27.9 us
    all_gather x2, blocking collectives, entering(): lax.all_gather(part.astype(kind), axis)  23.2 us
    dot_general x3, matrix products, body(): jnp.dot(columns, block_rows, preferred_element_type=jnp.float32)  17.1 us
    add x3, other arithmetic, combine_states(): return (earlier[0] * later[0], scale_state(earlier[1], later[0]) + later[1])  16 us
    dynamic_slice x8, local copies, waits for them, and re-layouts, body(): lax.map(lambda stretch_data: stretch_state(stretch_data[0], stretch_data[...  15.9 us
  transfers between devices with their start and end apart: 4, of which 4 were waited for; matrix products, arithmetic and copies ran while one was open for 12% of the time, Pallas kernels for 0%

commit v1 on v0

v1 whole, which is shorter than its diff:
```python
import functools

import jax
import jax.numpy as jnp
from jax import lax
from jax.experimental import pallas as pl
from jax.experimental.pallas import tpu as pltpu
from jax.sharding import Mesh
from jax.sharding import PartitionSpec as P

L = 256
CHUNK = 128
WIDE = 256
SEQ = ("seq_0", "seq_1", "seq_2")
LOG2E = 1.4426950408889634
F32 = jnp.float32
BF16 = jnp.bfloat16


def dot(a, b):
    return jnp.dot(a, b, preferred_element_type=F32)


def dot_lanes(a, b):
    return lax.dot_general(a, b, (((1,), (1,)), ((), ())), preferred_element_type=F32)


def iota(shape, dim):
    return lax.broadcasted_iota(jnp.int32, shape, dim)


def split3(x):
    hi = x.astype(BF16).astype(F32)
    mid = (x - hi).astype(BF16).astype(F32)
    return hi, mid, x - hi - mid


def packed3(x):
    hi, mid, lo = split3(x)
    low_lanes = iota(x.shape, 1) < 64
    first = jnp.where(low_lanes, hi, pltpu.roll(mid, 64, 1))
    second = jnp.where(low_lanes, lo, 0.0)
    return jnp.concatenate([first.astype(BF16), second.astype(BF16)], axis=1)


def head_select(depth, first_head, lanes_per_head):
    k = iota((depth, WIDE), 0)
    l = iota((depth, WIDE), 1)
    hit = ((k & 63) == first_head + l // lanes_per_head) & (k < 192)
    return jnp.where(hit, 1.0, 0.0).astype(BF16)


def state_kernel(dt_ref, bias_ref, rate_ref, used_ref, b_ref, inner_ref,
                 prior_ref, total_ref, pre_ref, cum_ref, row_ref, to_end, ends, b_turned):
    step = pl.program_id(0)
    rows = dt_ref.shape[0]
    chunks = rows // CHUNK

    @pl.when(step == 0)
    def _():
        v = dt_ref[...] + bias_ref[...]
        dt = jnp.maximum(v, 0.0) + jnp.log1p(jnp.exp(-jnp.abs(v)))
        slot = iota(dt.shape, 0) // L
        dt = dt * jnp.where(slot == 0, used_ref[0, 0], used_ref[0, 1])
        drop = dt * (rate_ref[...] * (-LOG2E))
        tri = jnp.where(iota((CHUNK, CHUNK), 0) >= iota((CHUNK, CHUNK), 1), 1.0, 0.0).astype(BF16)
        lasts = []
        for c in range(chunks):
            at = slice(c * CHUNK, (c + 1) * CHUNK)
            hi, mid, lo = split3(drop[at])
            cum = dot(tri, hi.astype(BF16)) + dot(tri, mid.astype(BF16)) + dot(tri, lo.astype(BF16))
            own = cum - jnp.log2(dt[at])
            last = cum[CHUNK - 1:CHUNK]
            lasts.append(last)
            cum_ref[at, :] = packed3(cum)
            reach = jnp.exp2(last - own)
            reach_hi = reach.astype(BF16).astype(F32)
            reach_lo = pltpu.roll(reach - reach_hi, 64, 1)
            to_end[at, :] = jnp.where(iota(reach.shape, 1) < 64, reach_hi, reach_lo).astype(BF16)
            turned = own.T
            for g in range(row_ref.shape[0]):
                row_ref[g, :, at] = turned[4 * g:4 * g + 4]
            b_turned[c] = b_ref[at, :].astype(F32).T.astype(BF16)
        lasts = jnp.concatenate(lasts + [jnp.zeros((16 - chunks, CHUNK), F32)], axis=0)
        ends[...] = packed3(lasts)

    first_head = step * (WIDE // 64)
    reach = dot(to_end[...], head_select(CHUNK, first_head, 64))
    scaled = (inner_ref[...].astype(F32) * reach).astype(BF16)
    decay = jnp.exp2(dot(ends[...], head_select(2 * CHUNK, first_head, 64)))
    state, before = None, jnp.ones((1, WIDE), F32)
    for c in range(chunks):
        add = dot(b_turned[c], scaled[c * CHUNK:(c + 1) * CHUNK])
        here = decay[c:c + 1]
        if c == 0:
            state = add
        else:
            prior_ref[c - 1] = state
            state = state * here + add
        pre_ref[c:c + 1, :] = before
        before = before * here
    pre_ref[chunks:chunks + 1, :] = before
    total_ref[...] = state.astype(total_ref.dtype)


def output_kernel(cum_ref, row_ref, c_ref, b_ref, tokens_ref, inner_ref, cot_ref, gain_ref,
                  prior_ref, pre_ref, enter_ref, out_ref, grad_ref, gram, hide, sum_heads, combined, through):
    step = pl.program_id(0)
    rows = c_ref.shape[0]
    chunks = rows // CHUNK

    @pl.when(step == 0)
    def _():
        for c in range(chunks):
            at = slice(c * CHUNK, (c + 1) * CHUNK)
            gram[at, :] = dot_lanes(c_ref[at, :], b_ref[at, :])
        hide[...] = jnp.where(iota(hide.shape, 0) >= iota(hide.shape, 1), 0.0, -1e30)
        same = iota(sum_heads.shape, 0) // 64 == iota(sum_heads.shape, 1) // 64
        sum_heads[...] = jnp.where(same, 1.0, 0.0).astype(BF16)
        combined[...] = jnp.zeros_like(combined)
        through[...] = jnp.zeros_like(through)

    first_head = step * 4
    low_half = iota((CHUNK, CHUNK), 1) < 64
    spread = [dot(cum_ref[...], head_select(2 * CHUNK, first_head + 2 * p, CHUNK)) for p in range(2)]
    for c in range(chunks):
        at = slice(c * CHUNK, (c + 1) * CHUNK)
        entering = enter_ref[...] * pre_ref[c:c + 1, :]
        if c > 0:
            entering = entering + prior_ref[c - 1]
        state_low = entering.astype(BF16)
        from_state = dot(c_ref[at, :], state_low)
        gain_row = gain_ref[c * CHUNK // L:c * CHUNK // L + 1, :]
        scaled = []
        for p in range(2):
            lanes = slice(p * CHUNK, (p + 1) * CHUNK)
            cum0, cum1 = spread[p][at, :CHUNK], spread[p][at, CHUNK:]
            w0 = jnp.exp2(cum0 - row_ref[0, 2 * p:2 * p + 1, at] + hide[...])
            w1 = jnp.exp2(cum1 - row_ref[0, 2 * p + 1:2 * p + 2, at] + hide[...])
            dots = gram[at, :]
            mixing = jnp.concatenate([(dots * w0).astype(BF16), (dots * w1).astype(BF16)], axis=1)
            x = inner_ref[at, lanes]
            zero = jnp.zeros_like(x)
            heads = jnp.concatenate([jnp.where(low_half, x, zero), jnp.where(low_half, zero, x)], axis=0)
            growth = jnp.exp2(jnp.where(low_half, cum0, cum1))
            full = dot(mixing, heads) + from_state[:, lanes] * growth
            gain = gain_row[:, lanes]
            grad_out = cot_ref[at, lanes].astype(F32) * gain
            parts = jnp.concatenate([(full * full).astype(BF16), (grad_out * full).astype(BF16)], axis=1)
            sums = dot(parts, sum_heads[...])
            inverse = lax.rsqrt(sums[:, :CHUNK] * (1.0 / 64) + 1.0)
            normed = full * inverse
            out_ref[at, lanes] = (normed * gain).astype(BF16)
            grad = inverse * (grad_out - normed * (sums[:, CHUNK:] * inverse * (1.0 / 64)))
            inter = dot_lanes(grad.astype(BF16), heads)
            combined[at, :] += inter[:, :CHUNK] * w0 + inter[:, CHUNK:] * w1
            scaled.append((grad * growth).astype(BF16))
        through[at, :] += dot_lanes(jnp.concatenate(scaled, axis=1), state_low)

    @pl.when(step == pl.num_programs(0) - 1)
    def _():
        turned = []
        for c in range(chunks):
            at = slice(c * CHUNK, (c + 1) * CHUNK)
            grad_rows = dot(combined[at, :].astype(BF16), b_ref[at, :]) + through[at, :]
            turned.append(grad_rows.astype(BF16).astype(F32).T.astype(BF16))
        turned = jnp.concatenate(turned, axis=1)
        for k in range(grad_ref.shape[0] // CHUNK):
            at = slice(k * CHUNK, (k + 1) * CHUNK)
            grad_ref[at, :] = dot(turned, tokens_ref[:, at]).T.astype(grad_ref.dtype)


def whole(shape):
    return pl.BlockSpec(shape, lambda j: (0,) * len(shape))


def local_states(dt_raw, dt_bias, decay_rate, used, b_proj, inner):
    rows, width = inner.shape
    state_size = b_proj.shape[1]
    steps = width // WIDE
    chunks = rows // CHUNK
    pad = 128 - dt_bias.shape[0]
    bias = jnp.pad(dt_bias, (0, pad))[None]
    rate = jnp.pad(decay_rate, (0, pad))[None]
    columns = lambda r: pl.BlockSpec((r, WIDE), lambda j: (0, j))
    return pl.pallas_call(
        state_kernel,
        grid=(steps,),
        out_shape=(
            jax.ShapeDtypeStruct((chunks - 1, state_size, width), F32),
            jax.ShapeDtypeStruct((state_size, width), BF16),
            jax.ShapeDtypeStruct((8, width), F32),
            jax.ShapeDtypeStruct((rows, 2 * CHUNK), BF16),
            jax.ShapeDtypeStruct((steps, 4, rows), F32),
        ),
        in_specs=[
            whole((rows, 128)), whole((1, 128)), whole((1, 128)),
            pl.BlockSpec(memory_space=pltpu.SMEM),
            whole((rows, state_size)), columns(rows),
        ],
        out_specs=(
            pl.BlockSpec((chunks - 1, state_size, WIDE), lambda j: (0, 0, j)),
            columns(state_size), columns(8), whole((rows, 2 * CHUNK)), whole((steps, 4, rows)),
        ),
        scratch_shapes=[
            pltpu.VMEM((rows, CHUNK), BF16),
            pltpu.VMEM((16, 2 * CHUNK), BF16),
            pltpu.VMEM((chunks, state_size, CHUNK), BF16),
        ],
        name="states",
    )(dt_raw, bias, rate, used, b_proj, inner)


def local_outputs(cum, row, c_proj, b_proj, tokens, inner, cot, gain, prior, pre, entering):
    rows, width = inner.shape
    depth = tokens.shape[1]
    state_size = b_proj.shape[1]
    steps = width // WIDE
    chunks = rows // CHUNK
    columns = lambda r: pl.BlockSpec((r, WIDE), lambda j: (0, j))
    return pl.pallas_call(
        output_kernel,
        grid=(steps,),
        out_shape=(
            jax.ShapeDtypeStruct((rows, width), BF16),
            jax.ShapeDtypeStruct((depth, state_size), BF16),
        ),
        in_specs=[
            whole((rows, 2 * CHUNK)), pl.BlockSpec((1, 4, rows), lambda j: (j, 0, 0)),
            whole((rows, state_size)), whole((rows, state_size)), whole((rows, depth)),
            columns(rows), columns(rows), columns(gain.shape[0]),
            pl.BlockSpec((chunks - 1, state_size, WIDE), lambda j: (0, 0, j)), columns(8), columns(state_size),
        ],
        out_specs=(columns(rows), whole((depth, state_size))),
        scratch_shapes=[
            pltpu.VMEM((rows, CHUNK), F32),
            pltpu.VMEM((CHUNK, CHUNK), F32),
            pltpu.VMEM((WIDE, WIDE), BF16),
            pltpu.VMEM((rows, CHUNK), F32),
            pltpu.VMEM((rows, CHUNK), F32),
        ],
        name="outputs",
    )(cum, row, c_proj, b_proj, tokens, inner, cot, gain, prior, pre, entering)


def entering_state(decay, state, axes):
    before = jnp.zeros(state.shape, F32)
    sub_decay, sub_state = decay, state.astype(F32)
    for axis in reversed(axes):
        peers, place = lax.axis_size(axis), lax.axis_index(axis)
        decays = lax.all_gather(sub_decay, axis)
        states = lax.all_gather(sub_state.astype(BF16), axis)
        inside_d, inside_s = jnp.ones_like(decay), jnp.zeros(state.shape, F32)
        sub_decay, sub_state = jnp.ones_like(decay), jnp.zeros(state.shape, F32)
        own_d, own_s = sub_decay, sub_state
        for k in range(peers):
            own_d = jnp.where(k == place, sub_decay, own_d)
            own_s = jnp.where(k == place, sub_state, own_s)
            sub_state = sub_state * decays[k] + states[k].astype(F32)
            sub_decay = sub_decay * decays[k]
        inside_d, inside_s = own_d, own_s
        if axis == axes[-1]:
            total_d, before = inside_d, inside_s
        else:
            before = inside_s * total_d + before
            total_d = inside_d * total_d
    return before


def cut_along(shard, dim, peers):
    shape = shard.shape
    blocks = shard.reshape(*shape[:dim], peers, shape[dim] // peers, *shape[dim + 1:])
    return jnp.moveaxis(blocks, dim, 0)


def sum_at_owner(shard, axis, dim):
    blocks = cut_along(shard, dim, lax.axis_size(axis))
    arrived = lax.all_to_all(blocks, axis, split_axis=0, concat_axis=0, tiled=True)
    return arrived.astype(F32).sum(axis=0)


def copy_for_each(shard, axis):
    peers = lax.axis_size(axis)
    return lax.all_to_all(jnp.broadcast_to(shard[None], (peers, *shard.shape)), axis, 0, 0, tiled=True)


def body(tokens, w_x, w_bc, w_dt, dt_bias, decay_rate, gain, cotangent, counts):
    seq_tokens = tokens[0]
    cot_rows = cotangent[0]
    slot_count = seq_tokens.shape[0] // L
    state_size = w_bc.shape[1] // 2
    group_index = lax.axis_index(SEQ)
    filled = jnp.sum(jnp.where(jnp.arange(counts.shape[0]) == group_index, counts, 0))
    slot_used = (jnp.arange(slot_count) < filled).astype(F32)
    pad = jnp.zeros((w_dt.shape[0], 128 - w_dt.shape[1]), BF16)
    pieces = lax.all_gather(jnp.concatenate([w_x, w_bc, w_dt, pad], axis=1), SEQ, axis=0, tiled=True)
    width = w_x.shape[1]
    inner = dot(seq_tokens, pieces[:, :width]).astype(BF16)
    bc_raw = dot(seq_tokens, pieces[:, width:width + 2 * state_size]).astype(BF16)
    dt_raw = dot(seq_tokens, pieces[:, width + 2 * state_size:])
    b_proj, c_proj = bc_raw[:, :state_size], bc_raw[:, state_size:]
    prior, total, pre, cum, row = local_states(dt_raw, dt_bias, decay_rate, slot_used[None], b_proj, inner)
    chunks = seq_tokens.shape[0] // CHUNK
    entering = entering_state(pre[chunks:chunks + 1], total, SEQ)
    gains = gain[None] * slot_used[:, None]
    outputs, grad = local_outputs(cum, row, c_proj, b_proj, seq_tokens, inner, cot_rows, gains, prior, pre, entering)
    partial_rows = sum_at_owner(grad, SEQ, 0)
    gradient = copy_for_each(partial_rows.astype(BF16), "dp").astype(F32).sum(axis=0)
    return (outputs[None], gradient)


def solution(mesh):
    finer = Mesh(mesh.devices.reshape(mesh.shape["dp"], 8, 2, 2), ("dp", "seq_0", "seq_1", "seq_2"))
    return jax.shard_map(
        body,
        mesh=finer,
        in_specs=(
            P("dp", SEQ, None), P(SEQ, None), P(SEQ, None), P(SEQ, None),
            P(), P(), P(), P("dp", SEQ, None), P(),
        ),
        out_specs=(P("dp", SEQ, None), P(SEQ, None)),
        check_vma=False,
    )
```

time: 471 us -> 398 us (0.85)
  local copies, waits for them, and re-layouts: 103 us -> 4.9 us
  other arithmetic: 60.1 us -> 14 us
  waiting for transfers between devices: 183 us -> 228 us
  Pallas kernels: 0 us -> 43.3 us
  matrix products: 42.9 us -> 18.5 us
  blocking collectives: 65.1 us -> 74.1 us
    mul x44 -> x0, local copies, waits for them, and re-layouts: 55.9 us -> none  [the longest x40 55.6 us: scale_state(): state.reshape(decay.shape[0], -1) * decay[:, None]]
    all_gather x4, waiting for transfers between devices: 183 us -> 228 us  [the longest x1 141 us: body(): lax.all_gather(jnp.concatenate([w_x, w_bc, w_dt, pad], axis=1), SEQ, axis...]
    pallas_call x0 -> x2, Pallas kernels: none -> 43.3 us  [the longest x1 32 us: local_outputs(): pl.pallas_call(output_kernel, grid=(steps,), out_shape=(jax.ShapeDtypeStr...]
    dot_general x18 -> x3, matrix products: 42.9 us -> 18.5 us  [dot(): return jnp.dot(a, b, preferred_element_type=F32)]
    dynamic_slice x10 -> x0, local copies, waits for them, and re-layouts: 17.2 us -> none  [the longest x8 15.9 us: body(): lax.map(lambda stretch_data: stretch_state(stretch_data[0], stretch_data[...]
    while x31 -> x0, local copies, waits for them, and re-layouts: 14.3 us -> none
    add x4 -> x1, other arithmetic: 17.9 us -> 4.62 us  [entering_state(): before = inside_s * total_d + before]
    mul x10 -> x3, other arithmetic: 12.9 us -> 0.72 us  [the longest x1 0.68 us: body(): gains = gain[None] * slot_used[:, None]]
  transfers between devices with their start and end apart: 4 -> 4, of which waited for: 4 -> 4; matrix products, arithmetic and copies ran while one was open for 12% -> 1% of each run, Pallas kernels for 0% -> 0%
where the time goes in v1:
time: 398 us; the launch traced here: 397 us
  waiting for transfers between devices  228 us (57%)
  blocking collectives  74.1 us (19%)
  Pallas kernels  43.3 us (11%)
  matrix products  18.5 us (5%)
  other arithmetic  14 us (4%)
  between operations  13.9 us (3%)
  local copies, waits for them, and re-layouts  4.9 us (1%)
    all_gather x1, waiting for transfers between devices, body(): lax.all_gather(jnp.concatenate([w_x, w_bc, w_dt, pad], axis=1), SEQ, axis...  141 us
    all_gather x3, waiting for transfers between devices, entering_state(): states = lax.all_gather(sub_state.astype(BF16), axis)  87 us
    all_gather x3, blocking collectives, entering_state(): decays = lax.all_gather(sub_decay, axis)  34.6 us
    pallas_call x1, Pallas kernels, local_outputs(): pl.pallas_call(output_kernel, grid=(steps,), out_shape=(jax.ShapeDtypeStr...  32 us
    all_to_all x1, blocking collectives, sum_at_owner(): lax.all_to_all(blocks, axis, split_axis=0, concat_axis=0, tiled=True)  27.9 us
    dot_general x3, matrix products, dot(): return jnp.dot(a, b, preferred_element_type=F32)  18.5 us
    all_to_all x1, blocking collectives, copy_for_each(): lax.all_to_all(jnp.broadcast_to(shard[None], (peers, *shard.shape)), axis...  11.6 us
    pallas_call x1, Pallas kernels, local_states(): pl.pallas_call(state_kernel, grid=(steps,), out_shape=(jax.ShapeDtypeStru...  11.3 us
  transfers between devices with their start and end apart: 4, of which 4 were waited for; matrix products, arithmetic and copies ran while one was open for 1% of the time, Pallas kernels for 0%

profile of v1, /device:TPU:4, one launch (start us, length us, event | category | flops | bytes accessed | tf_op | source)
XLA Modules:
  0.0 397.0 jit_solution(9250305752584818493)
XLA Ops:
  7.2 0.0 all-gather.10.cloned.1.call-start
  7.2 0.8 copy.19
  8.1 1.9 concatenate.3
  10.0 0.0 all-gather.16.cloned.1.call-start
  10.0 0.7 fusion.39
  10.7 1.3 compare_convert_fusion.1.used_ref
  12.0 0.5 pad_bitcast_fusion
  12.5 141.0 %all-gather.10.cloned.1.call-done = bf16[2560,3456]{1,0:T(8,128)(2,1)} async-done(((bf16[80,3456]{1,0:T(8,128)(2,1)}), bf16[2560,3456]{1,0:T(8,128)(2,1)}) %all-gather.10.cloned.1.call-update) | async-done | bytes 17694736 | tf_op jit(solution)/shard_map/all_gather | solution.py:296
  153.6 2.9 fusion.35
  156.5 0.7 fusion.43
  157.2 12.9 %fusion.5.inner_ref = bf16[512,3072]{1,0:T(8,128)(2,1)} fusion(bf16[2560,3456]{1,0:T(8,128)(2,1)} %all-gather.10.cloned.1.call-done, bf16[1,512,2560]{2,1,0:T(8,128)(2,1)S(1)} %copy-done.2), kind=kOutput, calls=%fused_computation.3 | convolution fusion | flops 8054636544 | bytes 21495808 | tf_op jit(solution)/shard_map/dot_general | solution.py:21
  170.2 2.6 convolution_bitcast_fusion.dt_ref
  172.8 11.3 %states.1 = (f32[3,128,3072]{2,1,0:T(8,128)}, bf16[128,3072]{1,0:T(8,128)(2,1)}, f32[8,3072]{1,0:T(8,128)}, bf16[512,256]{1,0:T(8,128)(2,1)}, f32[12,4,512]{2,1,0:T(4,128)}) custom-call(f32[512,128]{1,0:T(8,128)} %convolution_bitcast_fusion.dt_ref, f32[1,128]{1,0:T(1,128)} %get-tuple-element.34.bias_ref, f32[1,128]{1,0:T(1,128)} %get-tuple-element.33.rate_ref, ...), custom_call_target="tpu_custom_call" | custom-call | tf_op jit(solution)/shard_map/states/pallas_call | solution.py:186
  184.2 0.0 all-gather.12.cloned.1.call-start
  184.2 0.9 slice_bitcast_fusion.8
  185.1 1.8 all-gather.3
  187.0 11.6 %all-gather.16.cloned.1.call-done = bf16[256,3072]{1,0:T(8,128)(2,1)} async-done(((bf16[128,3072]{1,0:T(8,128)(2,1)}), bf16[256,3072]{1,0:T(8,128)(2,1)}) %all-gather.16.cloned.1.call-update) | async-done | bytes 1572880 | tf_op jit(solution)/shard_map/all_gather | solution.py:252
  198.6 2.5 fusion.19
  201.2 0.0 all-gather.14.cloned.1.call-start
  201.2 5.9 %all-gather.4 = f32[2,1,3072]{2,1,0:T(1,128)S(1)} all-gather(f32[1,1,3072]{2,1,0:T(1,128)S(1)} %get-tuple-element.30), channel_id=4, replica_groups=mesh['dp'=8,'seq_0'=8,'seq_1'=2,'seq_2'=2] {'seq_1'}, dimensions={0}, use_global_device_ids=true | all-gather | bytes 36864 | tf_op jit(solution)/shard_map/all_gather | solution.py:251
  207.2 26.6 %all-gather.12.cloned.1.call-done = bf16[2,128,3072]{2,1,0:T(8,128)(2,1)} async-done(((bf16[1,128,3072]{2,1,0:T(8,128)(2,1)}), bf16[2,128,3072]{2,1,0:T(8,128)(2,1)}) %all-gather.12.cloned.1.call-update) | async-done | bytes 1572880 | tf_op jit(solution)/shard_map/all_gather | solution.py:252
  233.8 2.7 fusion.10
  236.5 0.7 compare_convert_fusion
  237.2 0.7 broadcast_multiply_fusion.gain_ref
  237.9 26.9 %all_gather.35 = f32[8,1,3072]{2,1,0:T(1,128)S(1)} all-gather(f32[1,1,3072]{2,1,0:T(1,128)S(1)} %get-tuple-element.25), channel_id=1, replica_groups=mesh['dp'=8,'seq_0'=8,'seq_1'=2,'seq_2'=2] {'seq_0'}, dimensions={0}, use_global_device_ids=true | all-gather | bytes 110592 | tf_op jit(solution)/shard_map/all_gather | solution.py:251
  264.8 48.8 %all-gather.14.cloned.1.call-done = bf16[8,128,3072]{2,1,0:T(8,128)(2,1)} async-done(((bf16[1,128,3072]{2,1,0:T(8,128)(2,1)}), bf16[8,128,3072]{2,1,0:T(8,128)(2,1)}) %all-gather.14.cloned.1.call-update) | async-done | bytes 6291472 | tf_op jit(solution)/shard_map/all_gather | solution.py:252
  313.6 4.6 %fusion.15.enter_ref = f32[128,3072]{1,0:T(8,128)} fusion(bf16[8,128,3072]{2,1,0:T(8,128)(2,1)} %all-gather.14.cloned.1.call-done, f32[3072]{0:T(1024)S(1)} %bitcast.101, f32[3072]{0:T(1024)S(1)} %bitcast.105, f32[3072]{0:T(1024)S(1)} %bitcast.103, f32[3072]{0:T(1024)S(1)} %mul.190, f32[3072]{0:T(1024)S(1)} %bitcast.109, f32[3072]{0:T(1024)S(1)} %bitcast.110, ...), kind=kLoop, calls=%fused_computation.15 | loop fusion | flops 14548992 | bytes 8785929 | tf_op jit(solution)/shard_map/add | solution.py:265
  318.2 32.0 %outputs.1 = (bf16[512,3072]{1,0:T(8,128)(2,1)}, bf16[2560,128]{1,0:T(8,128)(2,1)}) custom-call(bf16[512,256]{1,0:T(8,128)(2,1)} %get-tuple-element.9.cum_ref, f32[12,4,512]{2,1,0:T(4,128)} %get-tuple-element.10.row_ref, bf16[512,128]{1,0:T(8,128)(2,1)} %get-tuple-element.16.c_ref, bf16[512,128]{1,0:T(8,128)(2,1)} %get-tuple-element.17.b_ref, ...), custom_call_target="tpu_custom_call" | custom-call | tf_op jit(solution)/shard_map/outputs/pallas_call | solution.py:221
  350.1 27.9 %all_to_all.10 = bf16[32,80,128]{2,1,0:T(8,128)(2,1)S(1)} all-to-all(bf16[32,80,128]{2,1,0:T(8,128)(2,1)} %bitcast.99), channel_id=1, replica_groups=mesh['dp'=8,'seq_0'=8,'seq_1'=2,'seq_2'=2] {'seq_0','seq_1','seq_2'}, dimensions={0} | all-to-all | bytes 1310720 | tf_op jit(solution)/shard_map/all_to_all | solution.py:278
  378.0 0.1 reduce_sum.31
  378.2 11.6 %all_to_all.11 = bf16[8,80,128]{2,1,0:T(8,128)(2,1)S(1)} all-to-all(bf16[8,80,128]{2,1,0:T(8,128)(2,1)S(1)} %broadcast_in_dim.30), channel_id=1, replica_groups=mesh['dp'=8,'seq_0'=8,'seq_1'=2,'seq_2'=2] {'dp'}, dimensions={0} | all-to-all | bytes 327680 | tf_op jit(solution)/shard_map/all_to_all | solution.py:284
  389.8 0.6 convert_reduce_fusion
  (24 shorter events, 0.2 us)
Async XLA Ops:
  7.2 2.9 copy-start.6
  7.2 4.8 %copy-start.5 = (f32[48]{0:T(128)S(1)}, f32[48]{0:T(128)}, u32[]{:S(2)}) copy-start(f32[48]{0:T(128)} %param.13) | copy-start | bytes 580
  7.2 4.8 %copy-start.4 = (f32[48]{0:T(128)S(1)}, f32[48]{0:T(128)}, u32[]{:S(2)}) copy-start(f32[48]{0:T(128)} %param.14) | copy-start | bytes 580
  7.2 146.4 %all-gather.10.cloned.1.call-start = ((), (), s32[]{:S(2)}) async-start(), calls=%async_computation.2 | async-start | bytes 18247680 | tf_op jit(solution)/shard_map/all_gather | solution.py:296
  10.0 188.7 %all-gather.16.cloned.1.call-start = ((), (), s32[]{:S(2)}) async-start(), calls=%async_computation.5 | async-start | bytes 2359296 | tf_op jit(solution)/shard_map/all_gather | solution.py:252
  12.5 144.7 %copy-start.2 = (bf16[1,512,2560]{2,1,0:T(8,128)(2,1)S(1)}, bf16[1,512,2560]{2,1,0:T(8,128)(2,1)}, u32[]{:S(2)}) copy-start(bf16[1,512,2560]{2,1,0:T(8,128)(2,1)} %param.9) | copy-start | bytes 7864324
  184.2 49.6 %all-gather.12.cloned.1.call-start = ((), (), s32[]{:S(2)}) async-start(), calls=%async_computation.3 | async-start | bytes 2359296 | tf_op jit(solution)/shard_map/all_gather | solution.py:252
  201.2 112.4 %all-gather.14.cloned.1.call-start = ((), (), s32[]{:S(2)}) async-start(), calls=%async_computation.4 | async-start | bytes 7077888 | tf_op jit(solution)/shard_map/all_gather | solution.py:252
  233.8 3.4 copy-start.3
  233.8 79.8 %copy-start = (bf16[256,3072]{1,0:T(8,128)(2,1)S(1)}, bf16[256,3072]{1,0:T(8,128)(2,1)}, u32[]{:S(2)}) copy-start(bf16[256,3072]{1,0:T(8,128)(2,1)} %all-gather.16.cloned.1.call-done) | copy-start | bytes 4718596
  233.8 79.8 %copy-start.1 = (bf16[2,128,3072]{2,1,0:T(8,128)(2,1)S(1)}, bf16[2,128,3072]{2,1,0:T(8,128)(2,1)}, u32[]{:S(2)}) copy-start(bf16[2,128,3072]{2,1,0:T(8,128)(2,1)} %all-gather.12.cloned.1.call-done) | copy-start | bytes 4718596
Sparse Core Ops, SparseCore 0:
  11.3 142.2 all-gather.9
  184.3 14.2 all-gather.15
  201.3 32.4 all-gather.11
  236.6 76.9 all-gather.13

commit v2 on v1

--- a/solution.py
+++ b/solution.py
@@ -11,7 +11,6 @@
 L = 256
 CHUNK = 128
 WIDE = 256
-SEQ = ("seq_0", "seq_1", "seq_2")
 LOG2E = 1.4426950408889634
 F32 = jnp.float32
 BF16 = jnp.bfloat16
@@ -51,7 +50,7 @@
 
 
 def state_kernel(dt_ref, bias_ref, rate_ref, used_ref, b_ref, inner_ref,
-                 prior_ref, total_ref, pre_ref, cum_ref, row_ref, to_end, ends, b_turned):
+                 prior_ref, total_ref, decay_ref, pre_ref, cum_ref, row_ref, to_end, ends, b_turned):
     step = pl.program_id(0)
     rows = dt_ref.shape[0]
     chunks = rows // CHUNK
@@ -99,8 +98,10 @@
             state = state * here + add
         pre_ref[c:c + 1, :] = before
         before = before * here
-    pre_ref[chunks:chunks + 1, :] = before
-    total_ref[...] = state.astype(total_ref.dtype)
+    for p in range(WIDE // CHUNK):
+        lanes = slice(p * CHUNK, (p + 1) * CHUNK)
+        total_ref[p] = state[:, lanes].astype(total_ref.dtype)
+        decay_ref[pl.ds(step * (WIDE // CHUNK) + p, 1), :] = before[:, lanes]
 
 
 def output_kernel(cum_ref, row_ref, c_ref, b_ref, tokens_ref, inner_ref, cot_ref, gain_ref,
@@ -123,9 +124,10 @@
     first_head = step * 4
     low_half = iota((CHUNK, CHUNK), 1) < 64
     spread = [dot(cum_ref[...], head_select(2 * CHUNK, first_head + 2 * p, CHUNK)) for p in range(2)]
+    entry = jnp.concatenate([enter_ref[p].astype(F32) for p in range(2)], axis=1)
     for c in range(chunks):
         at = slice(c * CHUNK, (c + 1) * CHUNK)
-        entering = enter_ref[...] * pre_ref[c:c + 1, :]
+        entering = entry * pre_ref[c:c + 1, :]
         if c > 0:
             entering = entering + prior_ref[c - 1]
         state_low = entering.astype(BF16)
@@ -170,6 +172,213 @@
             grad_ref[at, :] = dot(turned, tokens_ref[:, at]).T.astype(grad_ref.dtype)
 
 
+MESH = pl.DeviceIdType.MESH
+ZS = 8
+CLASSES = {"A": 0, "B": 1, "X": 2, "D": 3}
+
+
+def place_of():
+    dp, seq = lax.axis_index("dp"), lax.axis_index("seq")
+    return dict(y=dp // 2, x_lo=lax.rem(dp, 2), z=seq // 4, x_hi=lax.rem(seq // 2, 2), core=lax.rem(seq, 2), seq=seq, dp=dp)
+
+
+def device_at(place, **new):
+    p = {**place, **new}
+    return (p["y"] * 2 + p["x_lo"], p["z"] * 4 + p["x_hi"] * 2 + p["core"])
+
+
+def neighbours(place):
+    z, y = place["z"], place["y"]
+    flip = 1 - place["x_lo"]
+    return dict(
+        zp=device_at(place, z=lax.rem(z + 1, ZS)), zm=device_at(place, z=lax.rem(z + ZS - 1, ZS)),
+        yp=device_at(place, y=lax.rem(y + 1, 4)), ym=device_at(place, y=lax.rem(y + 3, 4)),
+        xu=device_at(place, x_lo=flip, x_hi=1 - place["x_hi"]), xo=device_at(place, x_lo=flip),
+        partner=device_at(place, core=1 - place["core"]),
+    )
+
+
+def meet(devices):
+    barrier = pltpu.get_barrier_semaphore()
+    for d in devices:
+        pl.semaphore_signal(barrier, inc=1, device_id=d, device_id_type=MESH)
+    pl.semaphore_wait(barrier, len(devices))
+
+
+ORDER = (
+    ("A", -1, "0"), ("A", 1, "0"), ("X", 0, "u"), ("A", -1, "1"), ("A", 1, "1"), ("B", -1, "0"), ("D", 0, "u"),
+    ("A", -2, "0"), ("A", 2, "0"), ("X", 0, "o"), ("B", -1, "1"), ("B", 1, "0"), ("X", -1, "u"), ("A", -2, "1"),
+    ("A", 2, "1"), ("D", 0, "o"), ("B", -2, "0"), ("B", 1, "1"), ("X", 1, "u"), ("A", -3, "0"), ("A", 3, "0"),
+    ("C", 0, ""), ("X", -1, "o"), ("B", -2, "1"), ("B", 2, "0"), ("X", -2, "u"), ("A", -3, "1"), ("A", 3, "1"),
+    ("X", 1, "o"), ("B", 2, "1"), ("D", -1, "u"), ("X", 2, "u"), ("A", 4, "0"), ("X", -2, "o"), ("A", 4, "1"),
+    ("D", -2, "u"), ("D", -1, "o"), ("D", 1, "u"), ("X", 2, "o"), ("C", -1, ""), ("B", -3, "0"), ("B", -3, "1"),
+    ("X", -3, "u"), ("D", -2, "o"), ("B", 3, "0"), ("B", 3, "1"), ("X", 3, "u"), ("X", -3, "o"), ("C", -2, ""),
+    ("B", 4, "0"), ("D", 1, "o"), ("D", 2, "u"), ("X", 3, "o"), ("B", 4, "1"), ("D", -3, "u"), ("X", 4, "u"),
+    ("D", -3, "o"), ("D", 3, "u"), ("C", 1, ""), ("D", 2, "o"), ("D", 4, "u"), ("C", -3, ""), ("D", 3, "o"),
+    ("X", 4, "o"), ("C", 2, ""), ("C", 3, ""), ("D", 4, "o"), ("C", 4, ""),
+)
+
+
+def gather_kernel(wx_ref, rest_ref, tokens_ref, inner_ref, bc_ref, dt_ref,
+                  held, cut, total, own_sem, send_sem, in_sem, side_sem, shard_sem):
+    place = place_of()
+    near = neighbours(place)
+    core, x_lo, x_hi, z, y = (place[k] for k in ("core", "x_lo", "x_hi", "z", "y"))
+    me = place["seq"]
+    quarter = held.shape[3]
+    y_lo = lax.rem(y, 2)
+    depth = cut.shape[2]
+    width = wx_ref.shape[1]
+
+    loads = [pltpu.make_async_copy(wx_ref.at[:, pl.ds(q * quarter, quarter)], held.at[q, me], own_sem.at[q]) for q in range(3)]
+    tail = width - 3 * quarter
+    loads.append(pltpu.make_async_copy(wx_ref.at[:, pl.ds(3 * quarter, tail)], held.at[3, me, :, pl.ds(0, tail)], own_sem.at[3]))
+    loads.append(pltpu.make_async_copy(rest_ref, held.at[3, me, :, pl.ds(tail, quarter - tail)], own_sem.at[4]))
+    for c in loads:
+        c.start()
+    meet(list(near.values()))
+    for c in loads:
+        c.wait()
+
+    sent = []
+
+    def unit(cls, dz, r):
+        q = core * 2 + (y_lo if cls in "AX" else 1 - y_lo)
+        xh = x_hi if cls in "AB" else 1 - x_hi
+        return held.at[q, lax.rem(z + dz + ZS, ZS) * 4 + xh * 2 + r]
+
+    def index(cls, dz, r):
+        return CLASSES[cls] * 16 + (dz % ZS) * 2 + r
+
+    def send(cls, dz, r, device, as_cls, as_dz, sem):
+        ref = unit(cls, dz, r)
+        c = pltpu.make_async_remote_copy(
+            src_ref=ref, dst_ref=ref, send_sem=send_sem.at[len(sent)], recv_sem=sem.at[index(as_cls, as_dz, r)],
+            device_id=device, device_id_type=MESH)
+        c.start()
+        sent.append(c)
+
+    def arrive(cls, dz, r):
+        ref = unit(cls, dz, r)
+        pltpu.make_async_remote_copy(
+            src_ref=ref, dst_ref=ref, send_sem=send_sem.at[0], recv_sem=in_sem.at[index(cls, dz, r)],
+            device_id=near["partner"], device_id_type=MESH).wait_recv()
+
+    def aside(cls, dz, r):
+        send(cls, dz, r, near["partner"], cls, dz, side_sem)
+
+    def along_y(r):
+        return device_at(place, y=lax.rem(y + 5 - 2 * r, 4))
+
+    shard = held.at[:, me]
+    shard_copy = pltpu.make_async_remote_copy(
+        src_ref=shard, dst_ref=shard, send_sem=shard_sem.at[0], recv_sem=shard_sem.at[1],
+        device_id=near["partner"], device_id_type=MESH)
+    shard_copy.start()
+    r_u, r_o = x_lo, 1 - x_lo
+    send("A", 0, core, near["zp"], "A", -1, in_sem)
+    send("A", 0, core, near["zm"], "A", 1, in_sem)
+
+    for i in range(ZS):
+        cut[i] = tokens_ref[:, i * depth:(i + 1) * depth]
+    total[...] = jnp.zeros_like(total)
+
+    other = held.at[:, me + 1 - 2 * core]
+    pltpu.make_async_remote_copy(
+        src_ref=other, dst_ref=other, send_sem=shard_sem.at[0], recv_sem=shard_sem.at[1],
+        device_id=near["partner"], device_id_type=MESH).wait_recv()
+    send("A", 0, 1 - core, near["zp"], "A", -1, in_sem)
+    send("A", 0, 1 - core, near["zm"], "A", 1, in_sem)
+    send("A", 0, r_o, near["xu"], "X", 0, in_sem)
+    send("B", 0, r_o, near["xu"], "D", 0, in_sem)
+    first = set()
+    for kind, dz, which in ORDER:
+        if kind != "C":
+            r = {"0": 0, "1": 1, "u": r_u, "o": r_o}[which]
+            arrive(kind, dz, r)
+        pair_done = (kind, dz) in first
+        first.add((kind, dz))
+        if kind == "A":
+            if dz < 0 and (dz > -3 or r == 0):
+                send("A", dz, r, near["zp"], "A", dz - 1, in_sem)
+            if 0 < dz < 4 and (dz < 3 or r == 1):
+                send("A", dz, r, near["zm"], "A", dz + 1, in_sem)
+            send("A", dz, r, near["yp" if r == 0 else "ym"], "B", dz, in_sem)
+            if pair_done:
+                send("A", dz, r_o, near["xu"], "X", dz, in_sem)
+            aside("A", dz, r)
+        elif kind == "B":
+            if pair_done and dz % 2 == 0:
+                send("B", dz, r_o, near["xu"], "D", dz, in_sem)
+            aside("B", dz, r)
+        elif kind == "X":
+            if which == "u":
+                send("X", dz, r, near["xo"], "X", dz, in_sem)
+            if dz % 2 == 1:
+                send("X", dz, r, along_y(r), "D", dz, in_sem)
+            aside("X", dz, r)
+        elif kind == "D":
+            if which == "u" and dz % 2 == 0:
+                send("D", dz, r, near["xo"], "D", dz, in_sem)
+            aside("D", dz, r)
+        else:
+            for cls in ("AB" if dz else "") + "XD":
+                for r in (0, 1):
+                    q = (1 - core) * 2 + (y_lo if cls in "AX" else 1 - y_lo)
+                    xh = x_hi if cls in "AB" else 1 - x_hi
+                    ref = held.at[q, lax.rem(z + dz + ZS, ZS) * 4 + xh * 2 + r]
+                    pltpu.make_async_remote_copy(
+                        src_ref=ref, dst_ref=ref, send_sem=send_sem.at[0], recv_sem=side_sem.at[index(cls, dz, r)],
+                        device_id=near["partner"], device_id_type=MESH).wait_recv()
+            zq = lax.rem(z + dz + ZS, ZS)
+
+            @pl.loop(0, 4)
+            def _(q):
+                block = held[q, pl.ds(zq * 4, 4)].reshape(depth, quarter)
+                total[q] += dot(cut[zq], block)
+
+    for q in range(3):
+        inner_ref[:, q * quarter:(q + 1) * quarter] = total[q].astype(BF16)
+    inner_ref[:, 3 * quarter:] = total[3, :, :tail].astype(BF16)
+    bc_ref[...] = total[3, :, tail:tail + 256].astype(BF16)
+    dt_ref[...] = total[3, :, tail + 256:tail + 384]
+    shard_copy.wait_send()
+    for c in sent:
+        c.wait_send()
+
+
+def gather_project(w_x, w_bc, w_dt, tokens):
+    rows, depth = tokens.shape
+    width = w_x.shape[1]
+    quarter = (width + 512) // 4
+    pad = jnp.zeros((w_x.shape[0], 512 - w_bc.shape[1] - w_dt.shape[1]), BF16)
+    rest = jnp.concatenate([w_bc, w_dt, pad], axis=1)
+    vmem = pl.BlockSpec(memory_space=pltpu.VMEM)
+    hbm = pl.BlockSpec(memory_space=pltpu.HBM)
+    return pl.pallas_call(
+        gather_kernel,
+        out_shape=(
+            jax.ShapeDtypeStruct((rows, width), BF16),
+            jax.ShapeDtypeStruct((rows, 256), BF16),
+            jax.ShapeDtypeStruct((rows, 128), F32),
+        ),
+        in_specs=[hbm, hbm, vmem],
+        out_specs=(vmem, vmem, vmem),
+        scratch_shapes=[
+            pltpu.VMEM((4, 32, w_x.shape[0], quarter), BF16),
+            pltpu.VMEM((ZS, rows, depth // ZS), BF16),
+            pltpu.VMEM((4, rows, quarter), F32),
+            pltpu.SemaphoreType.DMA((5,)),
+            pltpu.SemaphoreType.DMA((160,)),
+            pltpu.SemaphoreType.DMA((64,)),
+            pltpu.SemaphoreType.DMA((64,)),
+            pltpu.SemaphoreType.DMA((2,)),
+        ],
+        compiler_params=pltpu.CompilerParams(collective_id=0, has_side_effects=True, vmem_limit_bytes=60 * 2**20),
+        name="gather_project",
+    )(w_x, rest, tokens)
+
+
 def whole(shape):
     return pl.BlockSpec(shape, lambda j: (0,) * len(shape))
 
@@ -188,7 +397,8 @@
         grid=(steps,),
         out_shape=(
             jax.ShapeDtypeStruct((chunks - 1, state_size, width), F32),
-            jax.ShapeDtypeStruct((state_size, width), BF16),
+            jax.ShapeDtypeStruct((width // CHUNK, state_size, CHUNK), BF16),
+            jax.ShapeDtypeStruct((width // CHUNK, CHUNK), F32),
             jax.ShapeDtypeStruct((8, width), F32),
             jax.ShapeDtypeStruct((rows, 2 * CHUNK), BF16),
             jax.ShapeDtypeStruct((steps, 4, rows), F32),
@@ -200,7 +410,8 @@
         ],
         out_specs=(
             pl.BlockSpec((chunks - 1, state_size, WIDE), lambda j: (0, 0, j)),
-            columns(state_size), columns(8), whole((rows, 2 * CHUNK)), whole((steps, 4, rows)),
+            pl.BlockSpec((WIDE // CHUNK, state_size, CHUNK), lambda j: (j, 0, 0)), whole((width // CHUNK, CHUNK)),
+            columns(8), whole((rows, 2 * CHUNK)), whole((steps, 4, rows)),
         ),
         scratch_shapes=[
             pltpu.VMEM((rows, CHUNK), BF16),
@@ -229,7 +440,8 @@
             whole((rows, 2 * CHUNK)), pl.BlockSpec((1, 4, rows), lambda j: (j, 0, 0)),
             whole((rows, state_size)), whole((rows, state_size)), whole((rows, depth)),
             columns(rows), columns(rows), columns(gain.shape[0]),
-            pl.BlockSpec((chunks - 1, state_size, WIDE), lambda j: (0, 0, j)), columns(8), columns(state_size),
+            pl.BlockSpec((chunks - 1, state_size, WIDE), lambda j: (0, 0, j)), columns(8),
+            pl.BlockSpec((WIDE // CHUNK, state_size, CHUNK), lambda j: (j, 0, 0)),
         ],
         out_specs=(columns(rows), whole((depth, state_size))),
         scratch_shapes=[
@@ -243,45 +455,183 @@
     )(cum, row, c_proj, b_proj, tokens, inner, cot, gain, prior, pre, entering)
 
 
-def entering_state(decay, state, axes):
-    before = jnp.zeros(state.shape, F32)
-    sub_decay, sub_state = decay, state.astype(F32)
-    for axis in reversed(axes):
-        peers, place = lax.axis_size(axis), lax.axis_index(axis)
-        decays = lax.all_gather(sub_decay, axis)
-        states = lax.all_gather(sub_state.astype(BF16), axis)
-        inside_d, inside_s = jnp.ones_like(decay), jnp.zeros(state.shape, F32)
-        sub_decay, sub_state = jnp.ones_like(decay), jnp.zeros(state.shape, F32)
-        own_d, own_s = sub_decay, sub_state
-        for k in range(peers):
-            own_d = jnp.where(k == place, sub_decay, own_d)
-            own_s = jnp.where(k == place, sub_state, own_s)
-            sub_state = sub_state * decays[k] + states[k].astype(F32)
-            sub_decay = sub_decay * decays[k]
-        inside_d, inside_s = own_d, own_s
-        if axis == axes[-1]:
-            total_d, before = inside_d, inside_s
-        else:
-            before = inside_s * total_d + before
-            total_d = inside_d * total_d
-    return before
-
-
-def cut_along(shard, dim, peers):
-    shape = shard.shape
-    blocks = shard.reshape(*shape[:dim], peers, shape[dim] // peers, *shape[dim + 1:])
-    return jnp.moveaxis(blocks, dim, 0)
-
-
-def sum_at_owner(shard, axis, dim):
-    blocks = cut_along(shard, dim, lax.axis_size(axis))
-    arrived = lax.all_to_all(blocks, axis, split_axis=0, concat_axis=0, tiled=True)
-    return arrived.astype(F32).sum(axis=0)
-
-
-def copy_for_each(shard, axis):
-    peers = lax.axis_size(axis)
-    return lax.all_to_all(jnp.broadcast_to(shard[None], (peers, *shard.shape)), axis, 0, 0, tiled=True)
+def remote(src, dst, send_sem, recv_sem, device):
+    return pltpu.make_async_remote_copy(
+        src_ref=src, dst_ref=dst, send_sem=send_sem, recv_sem=recv_sem, device_id=device, device_id_type=MESH)
+
+
+def exchange_kernel(state_ref, decay_ref, enter_ref, decays, paired, across, own, arrived, leaving, gone, entry,
+                    d_send, d_recv, p_send, p_recv, x_send, x_recv, z_send, z_recv, e_send, e_recv):
+    place = place_of()
+    core, x_hi, z = place["core"], place["x_hi"], place["z"]
+    partner = device_at(place, core=1 - core)
+    column = device_at(place, x_hi=1 - x_hi)
+    corner = device_at(place, x_hi=1 - x_hi, core=1 - core)
+    up = device_at(place, z=lax.rem(z + 1, ZS))
+    down = device_at(place, z=lax.rem(z + ZS - 1, ZS))
+    half = state_ref.shape[0] // 2
+    mine, theirs = core * half, (1 - core) * half
+    member = x_hi * 2 + core
+
+    meet([partner, column, corner, up, down])
+    to_quad = [remote(decay_ref, decays.at[member], d_send.at[i], d_recv.at[i], d)
+               for i, d in enumerate((partner, column, corner))]
+    to_quad[0].start()
+    for i in range(half):
+        remote(state_ref.at[theirs + i], paired.at[i], p_send.at[i], p_recv.at[i], partner).start()
+    to_quad[1].start()
+    to_quad[2].start()
+    decays[member] = decay_ref[...]
+
+    @pl.when(z == 0)
+    def _():
+        arrived[...] = jnp.zeros_like(arrived)
+
+    for c, i in zip(to_quad, range(3)):
+        remote(decay_ref, decays.at[(member ^ (1, 2, 3)[i])], d_send.at[i], d_recv.at[i], partner).wait_recv()
+
+    def both_cores(i):
+        remote(paired.at[i], paired.at[i], p_send.at[i], p_recv.at[i], partner).wait_recv()
+
+    @pl.loop(0, half)
+    def _(i):
+        both_cores(i)
+        at = mine + i
+        own_state, other_state = state_ref[at].astype(F32), paired[i].astype(F32)
+        first = jnp.where(core == 0, own_state, other_state)
+        second = jnp.where(core == 0, other_state, own_state)
+        own[i] = (first * decays[x_hi * 2 + 1, pl.ds(at, 1), :] + second).astype(BF16)
+        remote(own.at[i], across.at[i], x_send.at[i], x_recv.at[i], column).start()
+
+    @pl.loop(0, half)
+    def _(i):
+        at = mine + i
+        d = [decays[m, pl.ds(at, 1), :] for m in range(4)]
+        remote(own.at[i], across.at[i], x_send.at[i], x_recv.at[i], column).wait_recv()
+        mine_t, other_t = own[i].astype(F32), across[i].astype(F32)
+        t0 = jnp.where(x_hi == 0, mine_t, other_t)
+        t1 = jnp.where(x_hi == 0, other_t, mine_t)
+        d0, d1 = d[0] * d[1], d[2] * d[3]
+
+        @pl.when(z > 0)
+        def _():
+            remote(arrived.at[i], arrived.at[i], z_send.at[i], z_recv.at[i], down).wait_recv()
+
+        before = arrived[i].astype(F32)
+
+        @pl.when(z < ZS - 1)
+        def _():
+            leaving[i] = (before * (d0 * d1) + (t0 * d1 + t1)).astype(BF16)
+            remote(leaving.at[i], arrived.at[i], z_send.at[i], z_recv.at[i], up).start()
+
+        here = jnp.where(x_hi == 0, before, before * d0 + t0)
+        first = jnp.where(core == 0, state_ref[at].astype(F32), paired[i].astype(F32))
+        after = here * jnp.where(x_hi == 0, d[0], d[2]) + first
+        entry[at] = jnp.where(core == 0, here, after).astype(BF16)
+        gone[i] = jnp.where(core == 0, after, here).astype(BF16)
+        remote(gone.at[i], entry.at[at], e_send.at[i], e_recv.at[i], partner).start()
+
+    @pl.loop(0, half)
+    def _(i):
+        remote(gone.at[i], entry.at[theirs + i], e_send.at[i], e_recv.at[i], partner).wait_recv()
+        remote(gone.at[i], entry.at[theirs + i], e_send.at[i], e_recv.at[i], partner).wait_send()
+        remote(own.at[i], across.at[i], x_send.at[i], x_recv.at[i], column).wait_send()
+        remote(paired.at[i], paired.at[i], p_send.at[i], p_recv.at[i], partner).wait_send()
+
+        @pl.when(z < ZS - 1)
+        def _():
+            remote(leaving.at[i], arrived.at[i], z_send.at[i], z_recv.at[i], up).wait_send()
+
+    for c in to_quad:
+        c.wait_send()
+    enter_ref[...] = entry[...]
+
+
+def entering_states(state, decay):
+    tiles = state.shape[0]
+    tile = state.shape[1:]
+    half = tiles // 2
+    vmem = pl.BlockSpec(memory_space=pltpu.VMEM)
+    sems = pltpu.SemaphoreType.DMA
+    return pl.pallas_call(
+        exchange_kernel,
+        out_shape=jax.ShapeDtypeStruct(state.shape, BF16),
+        in_specs=[vmem, vmem],
+        out_specs=vmem,
+        scratch_shapes=[pltpu.VMEM((4,) + decay.shape, F32)]
+        + [pltpu.VMEM((half,) + tile, BF16)] * 6
+        + [pltpu.VMEM(state.shape, BF16)]
+        + [sems((3,))] * 2 + [sems((half,))] * 8,
+        compiler_params=pltpu.CompilerParams(collective_id=1, has_side_effects=True),
+        name="entering_states",
+    )(state, decay)
+
+
+def reduce_kernel(part_ref, out_ref, paired, held, landed, own, copies, a_send, a_recv, b_send, b_recv, c_send, c_recv):
+    place = place_of()
+    core, dp = place["core"], place["dp"]
+    peers, parts = held.shape[0], copies.shape[0]
+    here = place["seq"] // 2
+    partner = device_at(place, core=1 - core)
+
+    def in_column(o):
+        b = lax.rem(here + o, peers)
+        return b, (dp, b * 2 + core)
+
+    def in_dp(o):
+        return (lax.rem(dp + o, parts), place["seq"])
+
+    meet([partner] + [in_column(o)[1] for o in range(1, peers)] + [in_dp(o) for o in range(1, parts)])
+    first = remote(part_ref.at[1 - core], paired, a_send, a_recv, partner)
+    first.start()
+    first.wait()
+    held[...] = (part_ref[core].astype(F32) + paired[...].astype(F32)).astype(BF16)
+    sent = []
+    for o in range(1, peers):
+        b, device = in_column(o)
+        c = remote(held.at[b], landed.at[o - 1], b_send.at[o - 1], b_recv.at[o - 1], device)
+        c.start()
+        sent.append(c)
+    total = held[here].astype(F32)
+    for o in range(1, peers):
+        sent[o - 1].wait_recv()
+        total = total + landed[o - 1].astype(F32)
+    own[...] = total.astype(BF16)
+    copies[dp] = own[...]
+    given = []
+    for o in range(1, parts):
+        c = remote(own, copies.at[dp], c_send.at[o - 1], c_recv.at[o - 1], in_dp(o))
+        c.start()
+        given.append(c)
+    for o in range(1, parts):
+        source = lax.rem(dp + parts - o, parts)
+        remote(own, copies.at[source], c_send.at[o - 1], c_recv.at[o - 1], in_dp(o)).wait_recv()
+    total = copies[0].astype(F32)
+    for i in range(1, parts):
+        total = total + copies[i].astype(F32)
+    out_ref[...] = total
+    for c in sent + given:
+        c.wait_send()
+
+
+def reduced_gradient(grad):
+    block = grad.shape[2:]
+    peers, parts = grad.shape[1], 8
+    vmem = pl.BlockSpec(memory_space=pltpu.VMEM)
+    sems = pltpu.SemaphoreType.DMA
+    return pl.pallas_call(
+        reduce_kernel,
+        out_shape=jax.ShapeDtypeStruct(block, F32),
+        in_specs=[vmem],
+        out_specs=vmem,
+        scratch_shapes=[
+            pltpu.VMEM((peers,) + block, BF16), pltpu.VMEM((peers,) + block, BF16),
+            pltpu.VMEM((peers - 1,) + block, BF16), pltpu.VMEM(block, BF16), pltpu.VMEM((parts,) + block, BF16),
+            sems, sems, sems((peers - 1,)), sems((peers - 1,)), sems((parts - 1,)), sems((parts - 1,)),
+        ],
+        compiler_params=pltpu.CompilerParams(collective_id=2, has_side_effects=True),
+        name="reduced_gradient",
+    )(grad)
 
 
 def body(tokens, w_x, w_bc, w_dt, dt_bias, decay_rate, gain, cotangent, counts):
@@ -289,35 +639,28 @@
     cot_rows = cotangent[0]
     slot_count = seq_tokens.shape[0] // L
     state_size = w_bc.shape[1] // 2
-    group_index = lax.axis_index(SEQ)
+    group_index = lax.axis_index("seq")
     filled = jnp.sum(jnp.where(jnp.arange(counts.shape[0]) == group_index, counts, 0))
     slot_used = (jnp.arange(slot_count) < filled).astype(F32)
-    pad = jnp.zeros((w_dt.shape[0], 128 - w_dt.shape[1]), BF16)
-    pieces = lax.all_gather(jnp.concatenate([w_x, w_bc, w_dt, pad], axis=1), SEQ, axis=0, tiled=True)
-    width = w_x.shape[1]
-    inner = dot(seq_tokens, pieces[:, :width]).astype(BF16)
-    bc_raw = dot(seq_tokens, pieces[:, width:width + 2 * state_size]).astype(BF16)
-    dt_raw = dot(seq_tokens, pieces[:, width + 2 * state_size:])
+    inner, bc_raw, dt_raw = gather_project(w_x, w_bc, w_dt, seq_tokens)
     b_proj, c_proj = bc_raw[:, :state_size], bc_raw[:, state_size:]
-    prior, total, pre, cum, row = local_states(dt_raw, dt_bias, decay_rate, slot_used[None], b_proj, inner)
-    chunks = seq_tokens.shape[0] // CHUNK
-    entering = entering_state(pre[chunks:chunks + 1], total, SEQ)
+    prior, total, decay, pre, cum, row = local_states(dt_raw, dt_bias, decay_rate, slot_used[None], b_proj, inner)
+    entering = entering_states(total, decay)
     gains = gain[None] * slot_used[:, None]
     outputs, grad = local_outputs(cum, row, c_proj, b_proj, seq_tokens, inner, cot_rows, gains, prior, pre, entering)
-    partial_rows = sum_at_owner(grad, SEQ, 0)
-    gradient = copy_for_each(partial_rows.astype(BF16), "dp").astype(F32).sum(axis=0)
+    rows = grad.shape[0] // 32
+    gradient = reduced_gradient(jnp.swapaxes(grad.reshape(16, 2, rows, state_size), 0, 1))
     return (outputs[None], gradient)
 
 
 def solution(mesh):
-    finer = Mesh(mesh.devices.reshape(mesh.shape["dp"], 8, 2, 2), ("dp", "seq_0", "seq_1", "seq_2"))
     return jax.shard_map(
         body,
-        mesh=finer,
+        mesh=mesh,
         in_specs=(
-            P("dp", SEQ, None), P(SEQ, None), P(SEQ, None), P(SEQ, None),
-            P(), P(), P(), P("dp", SEQ, None), P(),
+            P("dp", "seq", None), P("seq", None), P("seq", None), P("seq", None),
+            P(), P(), P(), P("dp", "seq", None), P(),
         ),
-        out_specs=(P("dp", SEQ, None), P(SEQ, None)),
+        out_specs=(P("dp", "seq", None), P("seq", None)),
         check_vma=False,
     )

time: 398 us -> 196 us (0.49)
  waiting for transfers between devices: 228 us -> 0 us
  Pallas kernels: 43.3 us -> 180 us
  blocking collectives: 74.1 us -> 0 us
  matrix products: 18.5 us -> 0 us
  between operations: 13.9 us -> 0.67 us
  other arithmetic: 14 us -> 5.9 us
    all_gather x4 -> x0, waiting for transfers between devices: 228 us -> none  [the longest x1 141 us: body(): lax.all_gather(jnp.concatenate([w_x, w_bc, w_dt, pad], axis=1), SEQ, axis...]
    pallas_call x0 -> x3, Pallas kernels: none -> 137 us  [the longest x1 72.8 us: gather_project(): pl.pallas_call(gather_kernel, out_shape=(jax.ShapeDtypeStruct((rows, widt...]
    all_to_all x2 -> x0, blocking collectives: 39.5 us -> none  [the longest x1 27.9 us: sum_at_owner(): lax.all_to_all(blocks, axis, split_axis=0, concat_axis=0, tiled=True)]
    all_gather x3 -> x0, blocking collectives: 34.6 us -> none  [entering_state(): decays = lax.all_gather(sub_decay, axis)]
    dot_general x3 -> x0, matrix products: 18.5 us -> none  [dot(): return jnp.dot(a, b, preferred_element_type=F32)]
    convert_element_type x2 -> x0, other arithmetic: 5.23 us -> none  [entering_state(): states = lax.all_gather(sub_state.astype(BF16), axis)]
    add x1 -> x0, other arithmetic: 4.62 us -> none  [entering_state(): before = inside_s * total_d + before]
  transfers between devices with their start and end apart: 4 -> 0, of which waited for: 4 -> 0; matrix products, arithmetic and copies ran while one was open for 1% -> 0% of each run, Pallas kernels for 0% -> 0%
where the time goes in v2:
time: 196 us; the launch traced here: 193 us
  Pallas kernels  180 us (92%)
  local copies, waits for them, and re-layouts  7.14 us (4%)
  other arithmetic  5.9 us (3%)
    pallas_call x1, Pallas kernels, gather_project(): pl.pallas_call(gather_kernel, out_shape=(jax.ShapeDtypeStruct((rows, widt...  72.8 us
    pallas_call x1, Pallas kernels, reduced_gradient(): pl.pallas_call(reduce_kernel, out_shape=jax.ShapeDtypeStruct(block, F32),...  42.6 us
    pallas_call x1, Pallas kernels, local_outputs(): pl.pallas_call(output_kernel, grid=(steps,), out_shape=(jax.ShapeDtypeStr...  31.9 us
    pallas_call x1, Pallas kernels, entering_states(): pl.pallas_call(exchange_kernel, out_shape=jax.ShapeDtypeStruct(state.shap...  21.1 us
    pallas_call x1, Pallas kernels, local_states(): pl.pallas_call(state_kernel, grid=(steps,), out_shape=(jax.ShapeDtypeStru...  11.3 us

profile of v2, /device:TPU:4, one launch (start us, length us, event | category | flops | bytes accessed | tf_op | source)
XLA Modules:
  0.0 193.5 jit_solution(535474722861407454)
XLA Ops:
  0.6 1.3 fusion
  1.9 0.6 compare_convert_fusion
  2.6 1.1 compare_convert_fusion.1.used_ref
  3.7 0.1 pad.11.clone
  3.8 1.2 pad_bitcast_fusion
  5.0 0.8 copy.12
  5.8 1.4 broadcast_multiply_fusion.gain_ref
  7.2 1.4 maximum_maximum_fusion.rest_ref
  8.6 72.8 %gather_project.1 = (bf16[512,3072]{1,0:T(8,128)(2,1)}, bf16[512,256]{1,0:T(8,128)(2,1)}, f32[512,128]{1,0:T(8,128)}) custom-call(bf16[80,3072]{1,0:T(8,128)(2,1)} %wx_ref.1, bf16[80,512]{1,0:T(8,128)(2,1)} %maximum_maximum_fusion.rest_ref, bf16[512,2560]{1,0:T(8,128)(2,1)} %bitcast.11), custom_call_target="tpu_custom_call" | custom-call | tf_op jit(solution)/shard_map/gather_project/pallas_call | solution.py:358
  81.4 1.7 fusion.1
  83.1 11.3 %states.1 = (f32[3,128,3072]{2,1,0:T(8,128)}, bf16[24,128,128]{2,1,0:T(8,128)(2,1)}, f32[24,128]{1,0:T(8,128)}, f32[8,3072]{1,0:T(8,128)}, bf16[512,256]{1,0:T(8,128)(2,1)}, /*index=5*/f32[12,4,512]{2,1,0:T(4,128)}) custom-call(f32[512,128]{1,0:T(8,128)} %get-tuple-element.13.dt_ref, f32[1,128]{1,0:T(1,128)} %get-tuple-element.27.bias_ref, ...), custom_call_target="tpu_custom_call" | custom-call | tf_op jit(solution)/shard_map/states/pallas_call | solution.py:395
  94.4 21.1 %entering_states.1.enter_ref = bf16[24,128,128]{2,1,0:T(8,128)(2,1)} custom-call(bf16[24,128,128]{2,1,0:T(8,128)(2,1)} %get-tuple-element.20.state_ref, f32[24,128]{1,0:T(8,128)} %get-tuple-element.21.decay_ref), custom_call_target="tpu_custom_call" | custom-call | tf_op jit(solution)/shard_map/entering_states/pallas_call | solution.py:556
  115.6 31.9 %outputs.1 = (bf16[512,3072]{1,0:T(8,128)(2,1)}, bf16[2560,128]{1,0:T(8,128)(2,1)}) custom-call(bf16[512,256]{1,0:T(8,128)(2,1)} %get-tuple-element.16.cum_ref, f32[12,4,512]{2,1,0:T(4,128)} %get-tuple-element.17.row_ref, bf16[512,128]{1,0:T(8,128)(2,1)} %get-tuple-element.24.c_ref, bf16[512,128]{1,0:T(8,128)(2,1)} %get-tuple-element.25.b_ref, ...), custom_call_target="tpu_custom_call" | custom-call | tf_op jit(solution)/shard_map/outputs/pallas_call | solution.py:432
  147.5 2.0 %copy.15 = bf16[16,2,80,128]{3,2,0,1:T(8,128)(2,1)} copy(bf16[16,2,80,128]{3,2,1,0:T(8,128)(2,1)} %bitcast.15) | data formatting | bytes 1310720 | tf_op jit(solution)/shard_map/reshape | solution.py:652
  149.5 42.6 %reduced_gradient.1 = f32[80,128]{1,0:T(8,128)} custom-call(bf16[2,16,80,128]{3,2,1,0:T(8,128)(2,1)} %bitcast.14), custom_call_target="tpu_custom_call" | custom-call | tf_op jit(solution)/shard_map/reduced_gradient/pallas_call | solution.py:622
  192.1 1.4 copy.17
  (1 shorter events, 0.0 us)

commit v3 on v2

v3 whole, which is shorter than its diff:
```python
import functools

import jax
import jax.numpy as jnp
from jax import lax
from jax.experimental import pallas as pl
from jax.experimental.pallas import tpu as pltpu
from jax.sharding import Mesh
from jax.sharding import PartitionSpec as P

L = 256
CHUNK = 128
WIDE = 256
LOG2E = 1.4426950408889634
F32 = jnp.float32
BF16 = jnp.bfloat16


def dot(a, b):
    return jnp.dot(a, b, preferred_element_type=F32)


def dot_lanes(a, b):
    return lax.dot_general(a, b, (((1,), (1,)), ((), ())), preferred_element_type=F32)


def iota(shape, dim):
    return lax.broadcasted_iota(jnp.int32, shape, dim)


def split3(x):
    hi = x.astype(BF16).astype(F32)
    mid = (x - hi).astype(BF16).astype(F32)
    return hi, mid, x - hi - mid


def packed3(x):
    hi, mid, lo = split3(x)
    low_lanes = iota(x.shape, 1) < 64
    first = jnp.where(low_lanes, hi, pltpu.roll(mid, 64, 1))
    second = jnp.where(low_lanes, lo, 0.0)
    return jnp.concatenate([first.astype(BF16), second.astype(BF16)], axis=1)


def head_select(depth, first_head, lanes_per_head, lanes=WIDE):
    k = iota((depth, lanes), 0)
    l = iota((depth, lanes), 1)
    hit = ((k & 63) == first_head + l // lanes_per_head) & (k < 192)
    return jnp.where(hit, 1.0, 0.0).astype(BF16)


def slots_used(counts_ref):
    filled = counts_ref[lax.axis_index("seq")]
    return [jnp.where(filled > k, 1.0, 0.0).astype(F32) for k in range(2)]


def decay_kernel(dt_ref, bias_ref, rate_ref, counts_ref, b_ref,
                 cum_ref, row_ref, to_end, b_turned, pre_ref, decay_ref, ends, padded):
    rows = dt_ref.shape[0]
    chunks = rows // CHUNK
    heads = bias_ref.shape[1]
    padded[...] = jnp.zeros_like(padded)
    padded[0:1, :heads] = bias_ref[...]
    padded[1:2, :heads] = rate_ref[...]
    used = slots_used(counts_ref)
    v = dt_ref[...] + padded[0:1, :]
    dt = jnp.maximum(v, 0.0) + jnp.log1p(jnp.exp(-jnp.abs(v)))
    slot = iota(dt.shape, 0) // L
    dt = dt * jnp.where(slot == 0, used[0], used[1])
    drop = dt * (padded[1:2, :] * (-LOG2E))
    tri = jnp.where(iota((CHUNK, CHUNK), 0) >= iota((CHUNK, CHUNK), 1), 1.0, 0.0).astype(BF16)
    lasts = []
    for c in range(chunks):
        at = slice(c * CHUNK, (c + 1) * CHUNK)
        hi, mid, lo = split3(drop[at])
        cum = dot(tri, hi.astype(BF16)) + dot(tri, mid.astype(BF16)) + dot(tri, lo.astype(BF16))
        own = cum - jnp.log2(dt[at])
        last = cum[CHUNK - 1:CHUNK]
        lasts.append(last)
        cum_ref[at, :] = packed3(cum)
        reach = jnp.exp2(last - own)
        reach_hi = reach.astype(BF16).astype(F32)
        reach_lo = pltpu.roll(reach - reach_hi, 64, 1)
        to_end[at, :] = jnp.where(iota(reach.shape, 1) < 64, reach_hi, reach_lo).astype(BF16)
        turned = own.T
        for g in range(row_ref.shape[0]):
            row_ref[g, :, at] = turned[2 * g:2 * g + 2]
        b_turned[c] = b_ref[at, :].astype(F32).T.astype(BF16)
    lasts = jnp.concatenate(lasts + [jnp.zeros((16 - chunks, CHUNK), F32)], axis=0)
    ends[...] = packed3(lasts)

    @pl.loop(0, pre_ref.shape[0])
    def _(j):
        decay = jnp.exp2(dot(ends[...], head_select(2 * CHUNK, 2 * j, 64, CHUNK)))
        before = jnp.ones((1, CHUNK), F32)
        for c in range(chunks):
            pre_ref[j, c:c + 1, :] = before
            before = before * decay[c:c + 1]
        pre_ref[j, chunks:2 * chunks, :] = decay[:chunks]
        decay_ref[pl.ds(j, 1), :] = before


def output_kernel(cum_ref, c_ref, b_ref, counts_ref, tokens_ref, inner_ref, cot_ref, gain_ref, intra_ref, weight_ref,
                  prior_ref, pre_ref, enter_ref, out_ref, grad_ref, sum_heads, combined, through, full_grad):
    step = pl.program_id(0)
    rows = c_ref.shape[0]
    chunks = rows // CHUNK

    @pl.when(step == 0)
    def _():
        same = iota(sum_heads.shape, 0) // 64 == iota(sum_heads.shape, 1) // 64
        sum_heads[...] = jnp.where(same, 1.0, 0.0).astype(BF16)
        combined[...] = jnp.zeros_like(combined)
        through[...] = jnp.zeros_like(through)

    used = slots_used(counts_ref)
    low_half = iota((CHUNK, CHUNK), 1) < 64
    growths = jnp.exp2(dot(cum_ref[...], head_select(2 * CHUNK, step * 4, 64)))
    entry = jnp.concatenate([enter_ref[p].astype(F32) for p in range(2)], axis=1)
    for c in range(chunks):
        at = slice(c * CHUNK, (c + 1) * CHUNK)
        entering = entry * jnp.concatenate([pre_ref[p, c:c + 1, :] for p in range(2)], axis=1)
        if c > 0:
            entering = entering + jnp.concatenate([prior_ref[p, c - 1] for p in range(2)], axis=1)
        state_low = entering.astype(BF16)
        from_state = dot(c_ref[at, :], state_low) * growths[at]
        gain_row = gain_ref[...] * used[c * CHUNK // L]
        scaled = []
        for p in range(2):
            lanes = slice(p * CHUNK, (p + 1) * CHUNK)
            x = inner_ref[at, lanes]
            zero = jnp.zeros_like(x)
            heads = jnp.concatenate([jnp.where(low_half, x, zero), jnp.where(low_half, zero, x)], axis=0)
            full = intra_ref[p, at, :] + from_state[:, lanes]
            gain = gain_row[:, lanes]
            grad_out = cot_ref[at, lanes].astype(F32) * gain
            parts = jnp.concatenate([(full * full).astype(BF16), (grad_out * full).astype(BF16)], axis=1)
            sums = dot(parts, sum_heads[...])
            inverse = lax.rsqrt(sums[:, :CHUNK] * (1.0 / 64) + 1.0)
            normed = full * inverse
            out_ref[at, lanes] = (normed * gain).astype(BF16)
            grad = inverse * (grad_out - normed * (sums[:, CHUNK:] * inverse * (1.0 / 64)))
            inter = dot_lanes(grad.astype(BF16), heads) * weight_ref[p, at, :].astype(F32)
            combined[at, :] += inter[:, :CHUNK] + inter[:, CHUNK:]
            scaled.append((grad * growths[at, lanes]).astype(BF16))
        through[at, :] += dot_lanes(jnp.concatenate(scaled, axis=1), state_low)

    @pl.when(step == pl.num_programs(0) - 1)
    def _():
        turned = []
        for c in range(chunks):
            at = slice(c * CHUNK, (c + 1) * CHUNK)
            grad_rows = dot(combined[at, :].astype(BF16), b_ref[at, :]) + through[at, :]
            turned.append(grad_rows.astype(BF16).astype(F32).T.astype(BF16))
        turned = jnp.concatenate(turned, axis=1)
        for k in range(full_grad.shape[0] // CHUNK):
            at = slice(k * CHUNK, (k + 1) * CHUNK)
            full_grad[at, :] = dot(turned, tokens_ref[:, at]).T.astype(BF16)
        block = grad_ref.shape[2]
        for k in range(full_grad.shape[0] // block):
            grad_ref[k % 2, k // 2] = full_grad[k * block:(k + 1) * block, :]


MESH = pl.DeviceIdType.MESH
ZS = 8
CLASSES = {"A": 0, "B": 1, "X": 2, "D": 3}


def place_of():
    dp, seq = lax.axis_index("dp"), lax.axis_index("seq")
    return dict(y=dp // 2, x_lo=lax.rem(dp, 2), z=seq // 4, x_hi=lax.rem(seq // 2, 2), core=lax.rem(seq, 2), seq=seq, dp=dp)


def device_at(place, **new):
    p = {**place, **new}
    return (p["y"] * 2 + p["x_lo"], p["z"] * 4 + p["x_hi"] * 2 + p["core"])


def neighbours(place):
    z, y = place["z"], place["y"]
    flip = 1 - place["x_lo"]
    return dict(
        zp=device_at(place, z=lax.rem(z + 1, ZS)), zm=device_at(place, z=lax.rem(z + ZS - 1, ZS)),
        yp=device_at(place, y=lax.rem(y + 1, 4)), ym=device_at(place, y=lax.rem(y + 3, 4)),
        xu=device_at(place, x_lo=flip, x_hi=1 - place["x_hi"]), xo=device_at(place, x_lo=flip),
        partner=device_at(place, core=1 - place["core"]),
    )


def meet(devices):
    barrier = pltpu.get_barrier_semaphore()
    for d in devices:
        pl.semaphore_signal(barrier, inc=1, device_id=d, device_id_type=MESH)
    pl.semaphore_wait(barrier, len(devices))


ORDER = (
    ("A", -1, "0"), ("A", 1, "0"), ("A", -1, "1"), ("A", 1, "1"), ("X", 0, "u"), ("B", -1, "0"), ("A", -2, "0"),
    ("A", 2, "0"), ("D", 0, "u"), ("B", 1, "0"), ("B", -1, "1"), ("X", 0, "o"), ("A", -2, "1"), ("A", 2, "1"),
    ("X", -1, "u"), ("B", -2, "0"), ("B", 1, "1"), ("D", 0, "o"), ("A", -3, "0"), ("A", 3, "0"), ("X", 1, "u"),
    ("B", -2, "1"), ("B", 2, "0"), ("X", -1, "o"), ("C", 0, ""), ("A", -3, "1"), ("A", 3, "1"), ("X", -2, "u"),
    ("B", 2, "1"), ("D", -1, "u"), ("X", 1, "o"), ("A", 4, "0"), ("X", 2, "u"), ("B", -3, "0"), ("D", -1, "o"),
    ("A", 4, "1"), ("X", -3, "u"), ("X", -2, "o"), ("C", -1, ""), ("D", -2, "u"), ("B", -3, "1"), ("B", 3, "0"),
    ("X", 2, "o"), ("X", 3, "u"), ("D", -2, "o"), ("B", 3, "1"), ("D", 1, "u"), ("X", -3, "o"), ("X", 4, "u"),
    ("C", -2, ""), ("B", 4, "0"), ("D", 1, "o"), ("D", -3, "u"), ("X", 3, "o"), ("D", 2, "u"), ("C", 1, ""),
    ("B", 4, "1"), ("D", 4, "u"), ("D", 3, "u"), ("X", 4, "o"), ("D", 2, "o"), ("D", -3, "o"), ("D", 4, "o"),
    ("C", 2, ""), ("D", 3, "o"), ("C", -3, ""), ("C", 4, ""), ("C", 3, ""),
)
FAR = ("x", "y", "z", "x", "y")


def gather_kernel(wx_ref, wbc_ref, wdt_ref, tokens_ref, inner_ref, b_ref, c_ref, dt_ref,
                  held, cut, total, own_sem, send_sem, in_sem, side_sem, shard_sem):
    place = place_of()
    near = neighbours(place)
    core, x_lo, x_hi, z, y = (place[k] for k in ("core", "x_lo", "x_hi", "z", "y"))
    me = place["seq"]
    quarter = held.shape[3]
    y_lo = lax.rem(y, 2)
    depth = cut.shape[2]
    width = wx_ref.shape[1]

    loads = [pltpu.make_async_copy(wx_ref.at[:, pl.ds(q * quarter, quarter)], held.at[q, me], own_sem.at[q]) for q in range(3)]
    tail = width - 3 * quarter
    loads.append(pltpu.make_async_copy(wx_ref.at[:, pl.ds(3 * quarter, tail)], held.at[3, me, :, pl.ds(0, tail)], own_sem.at[3]))
    loads.append(pltpu.make_async_copy(wbc_ref, held.at[3, me, :, pl.ds(tail, wbc_ref.shape[1])], own_sem.at[4]))
    for c in loads:
        c.start()
    spare = quarter - tail - wbc_ref.shape[1] - wdt_ref.shape[1]
    held[3, me, :, tail + wbc_ref.shape[1]:] = jnp.concatenate(
        [wdt_ref[...].astype(F32), jnp.zeros((wdt_ref.shape[0], spare), F32)], axis=1).astype(BF16)
    meet(list(near.values()))
    for c in loads:
        c.wait()

    sent = []

    def unit(cls, dz, r):
        q = core * 2 + (y_lo if cls in "AX" else 1 - y_lo)
        xh = x_hi if cls in "AB" else 1 - x_hi
        return held.at[q, lax.rem(z + dz + ZS, ZS) * 4 + xh * 2 + r]

    def index(cls, dz, r):
        return CLASSES[cls] * 16 + (dz % ZS) * 2 + r

    def send(cls, dz, r, device, as_cls, as_dz, sem):
        ref = unit(cls, dz, r)
        c = pltpu.make_async_remote_copy(
            src_ref=ref, dst_ref=ref, send_sem=send_sem.at[len(sent)], recv_sem=sem.at[index(as_cls, as_dz, r)],
            device_id=device, device_id_type=MESH)
        c.start()
        sent.append(c)

    def arrive(cls, dz, r):
        ref = unit(cls, dz, r)
        pltpu.make_async_remote_copy(
            src_ref=ref, dst_ref=ref, send_sem=send_sem.at[0], recv_sem=in_sem.at[index(cls, dz, r)],
            device_id=near["partner"], device_id_type=MESH).wait_recv()

    def aside(cls, dz, r):
        send(cls, dz, r, near["partner"], cls, dz, side_sem)

    def along_y(r):
        return device_at(place, y=lax.rem(y + 5 - 2 * r, 4))

    shard = held.at[:, me]
    shard_copy = pltpu.make_async_remote_copy(
        src_ref=shard, dst_ref=shard, send_sem=shard_sem.at[0], recv_sem=shard_sem.at[1],
        device_id=near["partner"], device_id_type=MESH)
    shard_copy.start()
    r_u, r_o = x_lo, 1 - x_lo
    send("A", 0, core, near["zp"], "A", -1, in_sem)
    send("A", 0, core, near["zm"], "A", 1, in_sem)

    for i in range(ZS):
        cut[i] = tokens_ref[:, i * depth:(i + 1) * depth]
    total[...] = jnp.zeros_like(total)

    other = held.at[:, me + 1 - 2 * core]
    pltpu.make_async_remote_copy(
        src_ref=other, dst_ref=other, send_sem=shard_sem.at[0], recv_sem=shard_sem.at[1],
        device_id=near["partner"], device_id_type=MESH).wait_recv()
    send("A", 0, 1 - core, near["zp"], "A", -1, in_sem)
    send("A", 0, 1 - core, near["zm"], "A", 1, in_sem)
    send("A", 0, r_o, near["xu"], "X", 0, in_sem)
    send("B", 0, r_o, near["xu"], "D", 0, in_sem)
    first = set()
    for kind, dz, which in ORDER:
        if kind != "C":
            r = {"0": 0, "1": 1, "u": r_u, "o": r_o}[which]
            arrive(kind, dz, r)
        pair_done = (kind, dz) in first
        first.add((kind, dz))
        if kind == "A":
            if dz < 0 and (dz > -3 or r == 0):
                send("A", dz, r, near["zp"], "A", dz - 1, in_sem)
            if 0 < dz < 4 and (dz < 3 or r == 1):
                send("A", dz, r, near["zm"], "A", dz + 1, in_sem)
            send("A", dz, r, near["yp" if r == 0 else "ym"], "B", dz, in_sem)
            if pair_done:
                send("A", dz, r_o, near["xu"], "X", dz, in_sem)
            aside("A", dz, r)
        elif kind == "B":
            if pair_done and FAR[abs(dz)] == "x":
                send("B", dz, r_o, near["xu"], "D", dz, in_sem)
            aside("B", dz, r)
        elif kind == "X":
            if which == "u":
                send("X", dz, r, near["xo"], "X", dz, in_sem)
            if FAR[abs(dz)] == "y":
                send("X", dz, r, along_y(r), "D", dz, in_sem)
            aside("X", dz, r)
        elif kind == "D":
            if which == "u" and FAR[abs(dz)] == "x":
                send("D", dz, r, near["xo"], "D", dz, in_sem)
            if -3 < dz <= 0 and FAR[abs(dz) + 1] == "z":
                send("D", dz, r, near["zp"], "D", dz - 1, in_sem)
            if 0 <= dz < 3 and FAR[abs(dz) + 1] == "z":
                send("D", dz, r, near["zm"], "D", dz + 1, in_sem)
            aside("D", dz, r)
        else:
            for cls in ("AB" if dz else "") + "XD":
                for r in (0, 1):
                    q = (1 - core) * 2 + (y_lo if cls in "AX" else 1 - y_lo)
                    xh = x_hi if cls in "AB" else 1 - x_hi
                    ref = held.at[q, lax.rem(z + dz + ZS, ZS) * 4 + xh * 2 + r]
                    pltpu.make_async_remote_copy(
                        src_ref=ref, dst_ref=ref, send_sem=send_sem.at[0], recv_sem=side_sem.at[index(cls, dz, r)],
                        device_id=near["partner"], device_id_type=MESH).wait_recv()
            zq = lax.rem(z + dz + ZS, ZS)

            @pl.loop(0, 4)
            def _(q):
                block = held[q, pl.ds(zq * 4, 4)].reshape(depth, quarter)
                total[q] += dot(cut[zq], block)

    for q in range(3):
        inner_ref[:, q * quarter:(q + 1) * quarter] = total[q].astype(BF16)
    inner_ref[:, 3 * quarter:] = total[3, :, :tail].astype(BF16)
    b_ref[...] = total[3, :, tail:tail + 128].astype(BF16)
    c_ref[...] = total[3, :, tail + 128:tail + 256].astype(BF16)
    dt_ref[...] = total[3, :, tail + 256:tail + 384]
    shard_copy.wait_send()
    for c in sent:
        c.wait_send()


def gather_project(w_x, w_bc, w_dt, tokens):
    rows, depth = tokens.shape
    width = w_x.shape[1]
    quarter = (width + 512) // 4
    vmem = pl.BlockSpec(memory_space=pltpu.VMEM)
    hbm = pl.BlockSpec(memory_space=pltpu.HBM)
    return pl.pallas_call(
        gather_kernel,
        out_shape=(
            jax.ShapeDtypeStruct((rows, width), BF16),
            jax.ShapeDtypeStruct((rows, 128), BF16),
            jax.ShapeDtypeStruct((rows, 128), BF16),
            jax.ShapeDtypeStruct((rows, 128), F32),
        ),
        in_specs=[hbm, hbm, vmem, vmem],
        out_specs=(vmem,) * 4,
        scratch_shapes=[
            pltpu.VMEM((4, 32, w_x.shape[0], quarter), BF16),
            pltpu.VMEM((ZS, rows, depth // ZS), BF16),
            pltpu.VMEM((4, rows, quarter), F32),
            pltpu.SemaphoreType.DMA((5,)),
            pltpu.SemaphoreType.DMA((160,)),
            pltpu.SemaphoreType.DMA((64,)),
            pltpu.SemaphoreType.DMA((64,)),
            pltpu.SemaphoreType.DMA((2,)),
        ],
        compiler_params=pltpu.CompilerParams(collective_id=0, has_side_effects=True, vmem_limit_bytes=67043328),
        name="gather_project",
    )(w_x, w_bc, w_dt, tokens)


def whole(shape):
    return pl.BlockSpec(shape, lambda j: (0,) * len(shape))


def local_decays(dt_raw, dt_bias, decay_rate, counts, b_proj, tiles):
    rows, state_size = b_proj.shape
    chunks = rows // CHUNK
    vmem = pl.BlockSpec(memory_space=pltpu.VMEM)
    return pl.pallas_call(
        decay_kernel,
        out_shape=(
            jax.ShapeDtypeStruct((rows, 2 * CHUNK), BF16),
            jax.ShapeDtypeStruct((tiles, 2, rows), F32),
            jax.ShapeDtypeStruct((rows, CHUNK), BF16),
            jax.ShapeDtypeStruct((chunks, state_size, CHUNK), BF16),
            jax.ShapeDtypeStruct((tiles, 2 * chunks, CHUNK), F32),
            jax.ShapeDtypeStruct((tiles, CHUNK), F32),
        ),
        in_specs=[vmem, vmem, vmem, pl.BlockSpec(memory_space=pltpu.SMEM), vmem],
        out_specs=(vmem,) * 6,
        scratch_shapes=[pltpu.VMEM((16, 2 * CHUNK), BF16), pltpu.VMEM((8, 128), F32)],
        name="decays",
    )(dt_raw, dt_bias[None], decay_rate[None], counts, b_proj)


def local_outputs(cum, c_proj, b_proj, counts, tokens, inner, cot, gain, intra, weight, prior, pre, entering):
    rows, width = inner.shape
    depth = tokens.shape[1]
    state_size = b_proj.shape[1]
    steps = width // WIDE
    chunks = rows // CHUNK
    owners = 32
    tiles = WIDE // CHUNK
    columns = lambda r: pl.BlockSpec((r, WIDE), lambda j: (0, j))
    tiled = lambda a, b: pl.BlockSpec((tiles, a, b), lambda j: (j, 0, 0))
    grad_shape = (2, owners // 2, depth // owners, state_size)
    return pl.pallas_call(
        output_kernel,
        grid=(steps,),
        out_shape=(
            jax.ShapeDtypeStruct((rows, width), BF16),
            jax.ShapeDtypeStruct(grad_shape, BF16),
        ),
        in_specs=[
            whole((rows, 2 * CHUNK)), whole((rows, state_size)), whole((rows, state_size)),
            pl.BlockSpec(memory_space=pltpu.SMEM), whole((rows, depth)),
            columns(rows), columns(rows), columns(1), tiled(rows, CHUNK), tiled(rows, WIDE),
            pl.BlockSpec((tiles, chunks - 1, state_size, CHUNK), lambda j: (j, 0, 0, 0)),
            tiled(2 * chunks, CHUNK), tiled(state_size, CHUNK),
        ],
        out_specs=(columns(rows), whole(grad_shape)),
        scratch_shapes=[
            pltpu.VMEM((WIDE, WIDE), BF16),
            pltpu.VMEM((rows, CHUNK), F32),
            pltpu.VMEM((rows, CHUNK), F32),
            pltpu.VMEM((depth, state_size), BF16),
        ],
        name="outputs",
    )(cum, c_proj, b_proj, counts, tokens, inner, cot, gain[None], intra, weight, prior, pre, entering)


def remote(src, dst, send_sem, recv_sem, device):
    return pltpu.make_async_remote_copy(
        src_ref=src, dst_ref=dst, send_sem=send_sem, recv_sem=recv_sem, device_id=device, device_id_type=MESH)


AHEAD = (2, 4)


def exchange_kernel(cum_in, row_in, reach_in, turned_in, pre_in, decay_ref, c_in, b_in, inner_in,
                    enter_ref, intra_ref, weight_ref, prior_ref,
                    cum_ref, row_ref, reach_ref, turned_ref, pre_ref, c_ref, b_ref, inner_ref, load_sem,
                    state, prior, s_done,
                    decays, paired, across, own, arrived, leaving, gone, entry, intra, weight, gram, hide, y_done, w_done,
                    d_send, d_recv, p_send, p_recv, x_send, x_recv, z_send, z_recv, e_send, e_recv):
    loads = [pltpu.make_async_copy(a, b, load_sem.at[i]) for i, (a, b) in enumerate((
        (inner_in, inner_ref), (reach_in, reach_ref), (turned_in, turned_ref), (pre_in, pre_ref),
        (cum_in, cum_ref), (row_in, row_ref), (c_in, c_ref), (b_in, b_ref)))]
    for c in loads:
        c.start()
    place = place_of()
    core, x_hi, z = place["core"], place["x_hi"], place["z"]
    partner = device_at(place, core=1 - core)
    column = device_at(place, x_hi=1 - x_hi)
    corner = device_at(place, x_hi=1 - x_hi, core=1 - core)
    up = device_at(place, z=lax.rem(z + 1, ZS))
    down = device_at(place, z=lax.rem(z + ZS - 1, ZS))
    half = state.shape[0] // 2
    chunks = prior.shape[1] + 1
    mine, theirs = core * half, (1 - core) * half
    member = x_hi * 2 + core

    meet([partner, column, corner, up, down])
    to_quad = [remote(decay_ref, decays.at[member], d_send.at[i], d_recv.at[i], d)
               for i, d in enumerate((partner, column, corner))]
    to_quad[0].start()
    to_quad[1].start()
    to_quad[2].start()
    for c in loads:
        c.wait()

    def pair_of(j):
        return inner_ref[:, pl.ds(pl.multiple_of(j * CHUNK, CHUNK), CHUNK)]

    def added(j):
        reach = dot(reach_ref[...], head_select(CHUNK, 2 * j, 64, CHUNK))
        scaled = (pair_of(j).astype(F32) * reach).astype(BF16)
        now = dot(turned_ref[0], scaled[:CHUNK])
        for c in range(1, chunks):
            prior[j, c - 1] = now
            now = now * pre_ref[j, chunks + c:chunks + c + 1, :] + dot(turned_ref[c], scaled[c * CHUNK:(c + 1) * CHUNK])
        pltpu.make_async_copy(prior.at[j], prior_ref.at[j], s_done.at[j]).start()
        state[j] = now.astype(BF16)

    @pl.loop(0, half)
    def _(i):
        added(theirs + i)
        remote(state.at[theirs + i], paired.at[i], p_send.at[i], p_recv.at[i], partner).start()

    decays[member] = decay_ref[...]

    @pl.when(z == 0)
    def _():
        arrived[...] = jnp.zeros_like(arrived)

    for c, i in zip(to_quad, range(3)):
        remote(decay_ref, decays.at[(member ^ (1, 2, 3)[i])], d_send.at[i], d_recv.at[i], partner).wait_recv()

    def both_cores(i):
        remote(paired.at[i], paired.at[i], p_send.at[i], p_recv.at[i], partner).wait_recv()

    @pl.loop(0, half)
    def _(i):
        at = mine + i
        added(at)
        both_cores(i)
        own_state, other_state = state[at].astype(F32), paired[i].astype(F32)
        first = jnp.where(core == 0, own_state, other_state)
        second = jnp.where(core == 0, other_state, own_state)
        own[i] = (first * decays[x_hi * 2 + 1, pl.ds(at, 1), :] + second).astype(BF16)
        remote(own.at[i], across.at[i], x_send.at[i], x_recv.at[i], column).start()

    for c in range(chunks):
        at = slice(c * CHUNK, (c + 1) * CHUNK)
        gram[at, :] = dot_lanes(c_ref[at, :], b_ref[at, :])
    hide[...] = jnp.where(iota(hide.shape, 0) >= iota(hide.shape, 1), 0.0, -1e30)
    tiles = intra.shape[0]

    def within(j):
        spread = dot(cum_ref[...], head_select(2 * CHUNK, 2 * j, CHUNK))
        low_half = iota((CHUNK, CHUNK), 1) < 64
        pair = pair_of(j)
        for c in range(chunks):
            at = slice(c * CHUNK, (c + 1) * CHUNK)
            w0 = jnp.exp2(spread[at, :CHUNK] - row_ref[j, 0:1, at] + hide[...])
            w1 = jnp.exp2(spread[at, CHUNK:] - row_ref[j, 1:2, at] + hide[...])
            dots = gram[at, :]
            mixing = jnp.concatenate([(dots * w0).astype(BF16), (dots * w1).astype(BF16)], axis=1)
            weight[j, at, :] = jnp.concatenate([w0.astype(BF16), w1.astype(BF16)], axis=1)
            x = pair[at]
            zero = jnp.zeros_like(x)
            heads = jnp.concatenate([jnp.where(low_half, x, zero), jnp.where(low_half, zero, x)], axis=0)
            intra[j, at, :] = dot(mixing, heads)
        pltpu.make_async_copy(intra.at[j], intra_ref.at[j], y_done.at[j]).start()
        pltpu.make_async_copy(weight.at[j], weight_ref.at[j], w_done.at[j]).start()

    ahead = jnp.minimum(AHEAD[0] + AHEAD[1] * z, tiles)
    pl.loop(0, ahead)(within)

    @pl.loop(0, half)
    def _(i):
        at = mine + i
        d = [decays[m, pl.ds(at, 1), :] for m in range(4)]
        remote(own.at[i], across.at[i], x_send.at[i], x_recv.at[i], column).wait_recv()
        mine_t, other_t = own[i].astype(F32), across[i].astype(F32)
        t0 = jnp.where(x_hi == 0, mine_t, other_t)
        t1 = jnp.where(x_hi == 0, other_t, mine_t)
        d0, d1 = d[0] * d[1], d[2] * d[3]

        @pl.when(z > 0)
        def _():
            remote(arrived.at[i], arrived.at[i], z_send.at[i], z_recv.at[i], down).wait_recv()

        before = arrived[i].astype(F32)

        @pl.when(z < ZS - 1)
        def _():
            leaving[i] = (before * (d0 * d1) + (t0 * d1 + t1)).astype(BF16)
            remote(leaving.at[i], arrived.at[i], z_send.at[i], z_recv.at[i], up).start()

        here = jnp.where(x_hi == 0, before, before * d0 + t0)
        first = jnp.where(core == 0, state[at].astype(F32), paired[i].astype(F32))
        after = here * jnp.where(x_hi == 0, d[0], d[2]) + first
        entry[at] = jnp.where(core == 0, here, after).astype(BF16)
        gone[i] = jnp.where(core == 0, after, here).astype(BF16)
        remote(gone.at[i], entry.at[at], e_send.at[i], e_recv.at[i], partner).start()

    pl.loop(ahead, tiles)(within)

    @pl.loop(0, tiles)
    def _(j):
        pltpu.make_async_copy(intra.at[j], intra_ref.at[j], y_done.at[j]).wait()
        pltpu.make_async_copy(weight.at[j], weight_ref.at[j], w_done.at[j]).wait()
        pltpu.make_async_copy(prior.at[j], prior_ref.at[j], s_done.at[j]).wait()

    @pl.loop(0, half)
    def _(i):
        remote(gone.at[i], entry.at[theirs + i], e_send.at[i], e_recv.at[i], partner).wait_recv()
        remote(gone.at[i], entry.at[theirs + i], e_send.at[i], e_recv.at[i], partner).wait_send()
        remote(own.at[i], across.at[i], x_send.at[i], x_recv.at[i], column).wait_send()
        remote(paired.at[i], paired.at[i], p_send.at[i], p_recv.at[i], partner).wait_send()

        @pl.when(z < ZS - 1)
        def _():
            remote(leaving.at[i], arrived.at[i], z_send.at[i], z_recv.at[i], up).wait_send()

    for c in to_quad:
        c.wait_send()
    enter_ref[...] = entry[...]


def entering_states(cum, row, reach, turned, pre, decay, c_proj, b_proj, inner):
    tiles = row.shape[0]
    half = tiles // 2
    rows = inner.shape[0]
    chunks, size, _ = turned.shape
    tile = (size, CHUNK)
    vmem = pl.BlockSpec(memory_space=pltpu.VMEM)
    hbm = pl.BlockSpec(memory_space=pltpu.HBM)
    sems = pltpu.SemaphoreType.DMA
    like = lambda a: pltpu.VMEM(a.shape, a.dtype)
    return pl.pallas_call(
        exchange_kernel,
        out_shape=(
            jax.ShapeDtypeStruct((tiles,) + tile, BF16),
            jax.ShapeDtypeStruct((tiles, rows, CHUNK), F32),
            jax.ShapeDtypeStruct((tiles, rows, 2 * CHUNK), BF16),
            jax.ShapeDtypeStruct((tiles, chunks - 1) + tile, F32),
        ),
        in_specs=[hbm] * 5 + [vmem] + [hbm] * 3,
        out_specs=(vmem, hbm, hbm, hbm),
        scratch_shapes=[like(a) for a in (cum, row, reach, turned, pre, c_proj, b_proj, inner)] + [
            sems((8,)), pltpu.VMEM((tiles,) + tile, BF16), pltpu.VMEM((tiles, chunks - 1) + tile, F32), sems((tiles,)),
            pltpu.VMEM((4,) + decay.shape, F32)]
        + [pltpu.VMEM((half,) + tile, BF16)] * 6
        + [
            pltpu.VMEM((tiles,) + tile, BF16),
            pltpu.VMEM((tiles, rows, CHUNK), F32), pltpu.VMEM((tiles, rows, 2 * CHUNK), BF16),
            pltpu.VMEM((rows, CHUNK), F32), pltpu.VMEM((CHUNK, CHUNK), F32), sems((tiles,)), sems((tiles,)),
        ]
        + [sems((3,))] * 2 + [sems((half,))] * 8,
        compiler_params=pltpu.CompilerParams(collective_id=1, has_side_effects=True, vmem_limit_bytes=67043328),
        name="entering_states",
    )(cum, row, reach, turned, pre, decay, c_proj, b_proj, inner)


def reduce_kernel(part_ref, out_ref, paired, held, landed, own, copies, a_send, a_recv, b_send, b_recv, c_send, c_recv):
    place = place_of()
    core, dp = place["core"], place["dp"]
    peers, parts = held.shape[0], copies.shape[0]
    here = place["seq"] // 2
    partner = device_at(place, core=1 - core)

    def in_column(o):
        b = lax.rem(here + o, peers)
        return b, (dp, b * 2 + core)

    def in_dp(o):
        return (lax.rem(dp + o, parts), place["seq"])

    meet([partner] + [in_column(o)[1] for o in range(1, peers)] + [in_dp(o) for o in range(1, parts)])
    first = remote(part_ref.at[1 - core], paired, a_send, a_recv, partner)
    first.start()
    first.wait()
    held[...] = (part_ref[core].astype(F32) + paired[...].astype(F32)).astype(BF16)
    sent = []
    for o in range(1, peers):
        b, device = in_column(o)
        c = remote(held.at[b], landed.at[o - 1], b_send.at[o - 1], b_recv.at[o - 1], device)
        c.start()
        sent.append(c)
    total = held[here].astype(F32)
    for o in range(1, peers):
        sent[o - 1].wait_recv()
        total = total + landed[o - 1].astype(F32)
    own[...] = total.astype(BF16)
    copies[dp] = own[...]
    given = []
    for o in range(1, parts):
        c = remote(own, copies.at[dp], c_send.at[o - 1], c_recv.at[o - 1], in_dp(o))
        c.start()
        given.append(c)
    for o in range(1, parts):
        source = lax.rem(dp + parts - o, parts)
        remote(own, copies.at[source], c_send.at[o - 1], c_recv.at[o - 1], in_dp(o)).wait_recv()
    total = copies[0].astype(F32)
    for i in range(1, parts):
        total = total + copies[i].astype(F32)
    out_ref[...] = total
    for c in sent + given:
        c.wait_send()


def reduced_gradient(grad):
    block = grad.shape[2:]
    peers, parts = grad.shape[1], 8
    vmem = pl.BlockSpec(memory_space=pltpu.VMEM)
    sems = pltpu.SemaphoreType.DMA
    return pl.pallas_call(
        reduce_kernel,
        out_shape=jax.ShapeDtypeStruct(block, F32),
        in_specs=[vmem],
        out_specs=vmem,
        scratch_shapes=[
            pltpu.VMEM((peers,) + block, BF16), pltpu.VMEM((peers,) + block, BF16),
            pltpu.VMEM((peers - 1,) + block, BF16), pltpu.VMEM(block, BF16), pltpu.VMEM((parts,) + block, BF16),
            sems, sems, sems((peers - 1,)), sems((peers - 1,)), sems((parts - 1,)), sems((parts - 1,)),
        ],
        compiler_params=pltpu.CompilerParams(collective_id=2, has_side_effects=True),
        name="reduced_gradient",
    )(grad)


def body(tokens, w_x, w_bc, w_dt, dt_bias, decay_rate, gain, cotangent, counts):
    seq_tokens = tokens[0]
    cot_rows = cotangent[0]
    inner, b_proj, c_proj, dt_raw = gather_project(w_x, w_bc, w_dt, seq_tokens)
    cum, row, reach, turned, pre, decay = local_decays(
        dt_raw, dt_bias, decay_rate, counts, b_proj, inner.shape[1] // CHUNK)
    entering, intra, weight, prior = entering_states(cum, row, reach, turned, pre, decay, c_proj, b_proj, inner)
    outputs, grad = local_outputs(
        cum, c_proj, b_proj, counts, seq_tokens, inner, cot_rows, gain, intra, weight, prior, pre, entering)
    gradient = reduced_gradient(grad)
    return (outputs[None], gradient)


def solution(mesh):
    return jax.shard_map(
        body,
        mesh=mesh,
        in_specs=(
            P("dp", "seq", None), P("seq", None), P("seq", None), P("seq", None),
            P(), P(), P(), P("dp", "seq", None), P(),
        ),
        out_specs=(P("dp", "seq", None), P("seq", None)),
        check_vma=False,
    )
```

time: 196 us -> 174 us (0.89)
  Pallas kernels: 180 us -> 170 us
  other arithmetic: 5.9 us -> 0 us
  local copies, waits for them, and re-layouts: 7.14 us -> 2.8 us
    pallas_call x1, Pallas kernels: 42.6 us -> 36.2 us  [reduced_gradient(): pl.pallas_call(reduce_kernel, out_shape=jax.ShapeDtypeStruct(block, F32),...]
    pallas_call x1, Pallas kernels: 31.9 us -> 25.6 us  [local_outputs(): pl.pallas_call(output_kernel, grid=(steps,), out_shape=(jax.ShapeDtypeStr...]
    pallas_call x2, Pallas kernels: 32.4 us -> 36.7 us  [the longest x1 30.7 us: entering_states(): pl.pallas_call(exchange_kernel, out_shape=(jax.ShapeDtypeStruct((tiles,)...]
    reshape x1 -> x0, local copies, waits for them, and re-layouts: 1.97 us -> none  [body(): grad.reshape(16, 2, rows, state_size)]
where the time goes in v3:
time: 174 us; the launch traced here: 173 us
  Pallas kernels  170 us (98%)
  local copies, waits for them, and re-layouts  2.8 us (2%)
    pallas_call x1, Pallas kernels, gather_project(): pl.pallas_call(gather_kernel, out_shape=(jax.ShapeDtypeStruct((rows, widt...  71.4 us
    pallas_call x1, Pallas kernels, reduced_gradient(): pl.pallas_call(reduce_kernel, out_shape=jax.ShapeDtypeStruct(block, F32),...  36.2 us
    pallas_call x1, Pallas kernels, entering_states(): pl.pallas_call(exchange_kernel, out_shape=(jax.ShapeDtypeStruct((tiles,)...  30.7 us
    pallas_call x1, Pallas kernels, local_outputs(): pl.pallas_call(output_kernel, grid=(steps,), out_shape=(jax.ShapeDtypeStr...  25.6 us
    pallas_call x1, Pallas kernels, local_decays(): pl.pallas_call(decay_kernel, out_shape=(jax.ShapeDtypeStruct((rows, 2 * C...  6.01 us

profile of v3, /device:TPU:4, one launch (start us, length us, event | category | flops | bytes accessed | tf_op | source)
XLA Modules:
  0.0 173.4 jit_solution(9791666604834069040)
XLA Ops:
  0.6 1.4 copy.11.wdt_ref
  2.0 71.4 %gather_project.1 = (bf16[512,3072]{1,0:T(8,128)(2,1)}, bf16[512,128]{1,0:T(8,128)(2,1)}, bf16[512,128]{1,0:T(8,128)(2,1)}, f32[512,128]{1,0:T(8,128)}) custom-call(bf16[80,3072]{1,0:T(8,128)(2,1)} %wx_ref.1, bf16[80,256]{1,0:T(8,128)(2,1)} %wbc_ref.1, bf16[80,48]{1,0:T(8,128)(2,1)} %copy.11.wdt_ref, bf16[512,2560]{1,0:T(8,128)(2,1)} %bitcast.6), custom_call_target="tpu_custom_call" | custom-call | tf_op jit(solution)/shard_map/gather_project/pallas_call | solution.py:354
  73.5 6.0 %decays.1 = (bf16[512,256]{1,0:T(8,128)(2,1)}, f32[24,2,512]{2,1,0:T(2,128)}, bf16[512,128]{1,0:T(8,128)(2,1)}, bf16[4,128,128]{2,1,0:T(8,128)(2,1)}, f32[24,8,128]{2,1,0:T(8,128)}, /*index=5*/f32[24,128]{1,0:T(8,128)}) custom-call(f32[512,128]{1,0:T(8,128)} %get-tuple-element.18.dt_ref, f32[1,48]{1,0:T(1,128)} %bitcast.10, f32[1,48]{1,0:T(1,128)} %bitcast.11, ...), custom_call_target="tpu_custom_call" | custom-call | tf_op jit(solution)/shard_map/decays/pallas_call | solution.py:387
  79.5 30.7 %entering_states.1 = (bf16[24,128,128]{2,1,0:T(8,128)(2,1)}, f32[24,512,128]{2,1,0:T(8,128)}, bf16[24,512,256]{2,1,0:T(8,128)(2,1)}, f32[24,3,128,128]{3,2,1,0:T(8,128)}) custom-call(bf16[512,256]{1,0:T(8,128)(2,1)} %get-tuple-element.20.cum_in.cum_ref, f32[24,2,512]{2,1,0:T(2,128)} %get-tuple-element.23.row_in, ...), custom_call_target="tpu_custom_call" | custom-call | tf_op jit(solution)/shard_map/entering_states/pallas_call | solution.py:610
  110.2 25.6 %outputs.1 = (bf16[512,3072]{1,0:T(8,128)(2,1)}, bf16[2,16,80,128]{3,2,1,0:T(8,128)(2,1)}) custom-call(bf16[512,256]{1,0:T(8,128)(2,1)} %get-tuple-element.20.cum_in.cum_ref, bf16[512,128]{1,0:T(8,128)(2,1)} %get-tuple-element.21.c_in.c_ref, bf16[512,128]{1,0:T(8,128)(2,1)} %get-tuple-element.19.b_ref.b_in, s32[32]{0:T(128)} %counts_ref.3, ...), custom_call_target="tpu_custom_call" | custom-call | tf_op jit(solution)/shard_map/outputs/pallas_call | solution.py:415
  135.7 36.2 %reduced_gradient.1 = f32[80,128]{1,0:T(8,128)} custom-call(bf16[2,16,80,128]{3,2,1,0:T(8,128)(2,1)} %get-tuple-element.33.part_ref), custom_call_target="tpu_custom_call" | custom-call | tf_op jit(solution)/shard_map/reduced_gradient/pallas_call | solution.py:687
  172.0 1.4 copy.13

commit v4 on v3

--- a/solution.py
+++ b/solution.py
@@ -55,7 +55,7 @@
 
 
 def decay_kernel(dt_ref, bias_ref, rate_ref, counts_ref, b_ref,
-                 cum_ref, row_ref, to_end, b_turned, pre_ref, decay_ref, ends, padded):
+                 cum_ref, row_ref, to_end, b_turned, pre_ref, decay_ref, padded):
     rows = dt_ref.shape[0]
     chunks = rows // CHUNK
     heads = bias_ref.shape[1]
@@ -86,18 +86,18 @@
         for g in range(row_ref.shape[0]):
             row_ref[g, :, at] = turned[2 * g:2 * g + 2]
         b_turned[c] = b_ref[at, :].astype(F32).T.astype(BF16)
-    lasts = jnp.concatenate(lasts + [jnp.zeros((16 - chunks, CHUNK), F32)], axis=0)
-    ends[...] = packed3(lasts)
-
-    @pl.loop(0, pre_ref.shape[0])
-    def _(j):
-        decay = jnp.exp2(dot(ends[...], head_select(2 * CHUNK, 2 * j, 64, CHUNK)))
-        before = jnp.ones((1, CHUNK), F32)
-        for c in range(chunks):
-            pre_ref[j, c:c + 1, :] = before
-            before = before * decay[c:c + 1]
-        pre_ref[j, chunks:2 * chunks, :] = decay[:chunks]
-        decay_ref[pl.ds(j, 1), :] = before
+    drops = [jnp.exp2(last) for last in lasts]
+    befores = [jnp.ones_like(drops[0])]
+    for d in drops[:-1]:
+        befores.append(befores[-1] * d)
+    by_head = jnp.concatenate(befores + drops, axis=0)
+    low_half = iota((2 * chunks, CHUNK), 1) < 64
+    for j in range(pre_ref.shape[0]):
+        low = jnp.broadcast_to(by_head[:, 2 * j:2 * j + 1], low_half.shape)
+        high = jnp.broadcast_to(by_head[:, 2 * j + 1:2 * j + 2], low_half.shape)
+        spread = jnp.where(low_half, low, high)
+        pre_ref[j] = spread
+        decay_ref[j:j + 1, :] = spread[chunks - 1:chunks] * spread[2 * chunks - 1:2 * chunks]
 
 
 def output_kernel(cum_ref, c_ref, b_ref, counts_ref, tokens_ref, inner_ref, cot_ref, gain_ref, intra_ref, weight_ref,
@@ -197,14 +197,15 @@
 ORDER = (
     ("A", -1, "0"), ("A", 1, "0"), ("A", -1, "1"), ("A", 1, "1"), ("X", 0, "u"), ("B", -1, "0"), ("A", -2, "0"),
     ("A", 2, "0"), ("D", 0, "u"), ("B", 1, "0"), ("B", -1, "1"), ("X", 0, "o"), ("A", -2, "1"), ("A", 2, "1"),
-    ("X", -1, "u"), ("B", -2, "0"), ("B", 1, "1"), ("D", 0, "o"), ("A", -3, "0"), ("A", 3, "0"), ("X", 1, "u"),
-    ("B", -2, "1"), ("B", 2, "0"), ("X", -1, "o"), ("C", 0, ""), ("A", -3, "1"), ("A", 3, "1"), ("X", -2, "u"),
-    ("B", 2, "1"), ("D", -1, "u"), ("X", 1, "o"), ("A", 4, "0"), ("X", 2, "u"), ("B", -3, "0"), ("D", -1, "o"),
-    ("A", 4, "1"), ("X", -3, "u"), ("X", -2, "o"), ("C", -1, ""), ("D", -2, "u"), ("B", -3, "1"), ("B", 3, "0"),
-    ("X", 2, "o"), ("X", 3, "u"), ("D", -2, "o"), ("B", 3, "1"), ("D", 1, "u"), ("X", -3, "o"), ("X", 4, "u"),
-    ("C", -2, ""), ("B", 4, "0"), ("D", 1, "o"), ("D", -3, "u"), ("X", 3, "o"), ("D", 2, "u"), ("C", 1, ""),
-    ("B", 4, "1"), ("D", 4, "u"), ("D", 3, "u"), ("X", 4, "o"), ("D", 2, "o"), ("D", -3, "o"), ("D", 4, "o"),
-    ("C", 2, ""), ("D", 3, "o"), ("C", -3, ""), ("C", 4, ""), ("C", 3, ""),
+    ("X", -1, "u"), ("B", -2, "0"), ("B", 1, "1"), ("D", 0, "o"), ("C", 0, "Q"), ("A", -3, "0"), ("A", 3, "0"),
+    ("X", 1, "u"), ("B", -2, "1"), ("B", 2, "0"), ("X", -1, "o"), ("C", 0, "R"), ("A", -3, "1"), ("A", 3, "1"),
+    ("X", -2, "u"), ("B", 2, "1"), ("D", -1, "u"), ("C", -1, "Q"), ("X", 2, "u"), ("A", 4, "0"), ("X", 1, "o"),
+    ("B", -3, "0"), ("D", -1, "o"), ("C", 1, "Q"), ("A", 4, "1"), ("X", -3, "u"), ("X", -2, "o"), ("D", -2, "u"),
+    ("C", -1, "R"), ("B", -3, "1"), ("B", 3, "0"), ("X", 2, "o"), ("X", 3, "u"), ("C", -2, "Q"), ("D", -2, "o"),
+    ("C", 2, "Q"), ("B", 3, "1"), ("D", 1, "u"), ("X", -3, "o"), ("X", 4, "u"), ("B", 4, "0"), ("D", 1, "o"),
+    ("C", -2, "R"), ("D", -3, "u"), ("X", 3, "o"), ("C", -3, "Q"), ("C", 1, "R"), ("B", 4, "1"), ("C", 3, "Q"),
+    ("D", 2, "u"), ("D", 4, "u"), ("D", 3, "u"), ("X", 4, "o"), ("D", 2, "o"), ("C", 4, "Q"), ("D", -3, "o"),
+    ("D", 3, "o"), ("D", 4, "o"), ("C", 2, "R"), ("C", -3, "R"), ("C", 3, "R"), ("C", 4, "R"),
 )
 FAR = ("x", "y", "z", "x", "y")
 
@@ -319,7 +320,8 @@
                 send("D", dz, r, near["zm"], "D", dz + 1, in_sem)
             aside("D", dz, r)
         else:
-            for cls in ("AB" if dz else "") + "XD":
+            own = which == "Q"
+            for cls in (("A" if own else "B") if dz else "") + ("X" if own else "D"):
                 for r in (0, 1):
                     q = (1 - core) * 2 + (y_lo if cls in "AX" else 1 - y_lo)
                     xh = x_hi if cls in "AB" else 1 - x_hi
@@ -329,8 +331,11 @@
                         device_id=near["partner"], device_id_type=MESH).wait_recv()
             zq = lax.rem(z + dz + ZS, ZS)
 
-            @pl.loop(0, 4)
-            def _(q):
+            quarters = y_lo if own else 1 - y_lo
+
+            @pl.loop(0, 2)
+            def _(i, quarters=quarters, zq=zq):
+                q = 2 * i + quarters
                 block = held[q, pl.ds(zq * 4, 4)].reshape(depth, quarter)
                 total[q] += dot(cut[zq], block)
 
@@ -396,7 +401,7 @@
         ),
         in_specs=[vmem, vmem, vmem, pl.BlockSpec(memory_space=pltpu.SMEM), vmem],
         out_specs=(vmem,) * 6,
-        scratch_shapes=[pltpu.VMEM((16, 2 * CHUNK), BF16), pltpu.VMEM((8, 128), F32)],
+        scratch_shapes=[pltpu.VMEM((8, 128), F32)],
         name="decays",
     )(dt_raw, dt_bias[None], decay_rate[None], counts, b_proj)
 
@@ -442,7 +447,7 @@
         src_ref=src, dst_ref=dst, send_sem=send_sem, recv_sem=recv_sem, device_id=device, device_id_type=MESH)
 
 
-AHEAD = (2, 4)
+LAG = (6, 4)
 
 
 def exchange_kernel(cum_in, row_in, reach_in, turned_in, pre_in, decay_ref, c_in, b_in, inner_in,
@@ -490,11 +495,6 @@
         pltpu.make_async_copy(prior.at[j], prior_ref.at[j], s_done.at[j]).start()
         state[j] = now.astype(BF16)
 
-    @pl.loop(0, half)
-    def _(i):
-        added(theirs + i)
-        remote(state.at[theirs + i], paired.at[i], p_send.at[i], p_recv.at[i], partner).start()
-
     decays[member] = decay_ref[...]
 
     @pl.when(z == 0)
@@ -507,10 +507,13 @@
     def both_cores(i):
         remote(paired.at[i], paired.at[i], p_send.at[i], p_recv.at[i], partner).wait_recv()
 
-    @pl.loop(0, half)
-    def _(i):
+    def leave(i):
+        added(theirs + i)
+        remote(state.at[theirs + i], paired.at[i], p_send.at[i], p_recv.at[i], partner).start()
+        added(mine + i)
+
+    def join(i):
         at = mine + i
-        added(at)
         both_cores(i)
         own_state, other_state = state[at].astype(F32), paired[i].astype(F32)
         first = jnp.where(core == 0, own_state, other_state)
@@ -542,11 +545,7 @@
         pltpu.make_async_copy(intra.at[j], intra_ref.at[j], y_done.at[j]).start()
         pltpu.make_async_copy(weight.at[j], weight_ref.at[j], w_done.at[j]).start()
 
-    ahead = jnp.minimum(AHEAD[0] + AHEAD[1] * z, tiles)
-    pl.loop(0, ahead)(within)
-
-    @pl.loop(0, half)
-    def _(i):
+    def chain(i):
         at = mine + i
         d = [decays[m, pl.ds(at, 1), :] for m in range(4)]
         remote(own.at[i], across.at[i], x_send.at[i], x_recv.at[i], column).wait_recv()
@@ -573,7 +572,27 @@
         gone[i] = jnp.where(core == 0, after, here).astype(BF16)
         remote(gone.at[i], entry.at[at], e_send.at[i], e_recv.at[i], partner).start()
 
-    pl.loop(ahead, tiles)(within)
+    lag = LAG[0] + LAG[1] * z
+    slots = half + tiles
+    length = jnp.maximum(slots, lag + half)
+
+    @pl.loop(0, length)
+    def _(slot):
+        @pl.when(slot < half)
+        def _():
+            leave(slot)
+
+        @pl.when((slot >= 2) & (slot < half + 2))
+        def _():
+            join(slot - 2)
+
+        @pl.when((slot >= half) & (slot < slots))
+        def _():
+            within(slot - half)
+
+        @pl.when((slot >= lag) & (slot < lag + half))
+        def _():
+            chain(slot - lag)
 
     @pl.loop(0, tiles)
     def _(j):

time: 174 us -> 168 us (0.966)
  Pallas kernels: 170 us -> 164 us
    pallas_call x1, Pallas kernels: 6.01 us -> 2.38 us  [local_decays(): pl.pallas_call(decay_kernel, out_shape=(jax.ShapeDtypeStruct((rows, 2 * C...]
    pallas_call x1, Pallas kernels: 71.4 us -> 68 us  [gather_project(): pl.pallas_call(gather_kernel, out_shape=(jax.ShapeDtypeStruct((rows, widt...]
    pallas_call x1, Pallas kernels: 30.7 us -> 32.5 us  [entering_states(): pl.pallas_call(exchange_kernel, out_shape=(jax.ShapeDtypeStruct((tiles,)...]
where the time goes in v4:
time: 168 us
  Pallas kernels  164 us (98%)
  local copies, waits for them, and re-layouts  2.8 us (2%)
    pallas_call x1, Pallas kernels, gather_project(): pl.pallas_call(gather_kernel, out_shape=(jax.ShapeDtypeStruct((rows, widt...  68 us
    pallas_call x1, Pallas kernels, reduced_gradient(): pl.pallas_call(reduce_kernel, out_shape=jax.ShapeDtypeStruct(block, F32),...  36.1 us
    pallas_call x1, Pallas kernels, entering_states(): pl.pallas_call(exchange_kernel, out_shape=(jax.ShapeDtypeStruct((tiles,)...  32.5 us
    pallas_call x1, Pallas kernels, local_outputs(): pl.pallas_call(output_kernel, grid=(steps,), out_shape=(jax.ShapeDtypeStr...  25.6 us

profile of v4, /device:TPU:4, one launch (start us, length us, event | category | flops | bytes accessed | tf_op | source)
XLA Modules:
  0.0 167.9 jit_solution(15848373687472914207)
XLA Ops:
  0.6 1.4 copy.11.wdt_ref
  2.0 68.0 %gather_project.1 = (bf16[512,3072]{1,0:T(8,128)(2,1)}, bf16[512,128]{1,0:T(8,128)(2,1)}, bf16[512,128]{1,0:T(8,128)(2,1)}, f32[512,128]{1,0:T(8,128)}) custom-call(bf16[80,3072]{1,0:T(8,128)(2,1)} %wx_ref.1, bf16[80,256]{1,0:T(8,128)(2,1)} %wbc_ref.1, bf16[80,48]{1,0:T(8,128)(2,1)} %copy.11.wdt_ref, bf16[512,2560]{1,0:T(8,128)(2,1)} %bitcast.6), custom_call_target="tpu_custom_call" | custom-call | tf_op jit(solution)/shard_map/gather_project/pallas_call | solution.py:359
  70.0 2.4 %decays.1 = (bf16[512,256]{1,0:T(8,128)(2,1)}, f32[24,2,512]{2,1,0:T(2,128)}, bf16[512,128]{1,0:T(8,128)(2,1)}, bf16[4,128,128]{2,1,0:T(8,128)(2,1)}, f32[24,8,128]{2,1,0:T(8,128)}, /*index=5*/f32[24,128]{1,0:T(8,128)}) custom-call(f32[512,128]{1,0:T(8,128)} %get-tuple-element.18.dt_ref, f32[1,48]{1,0:T(1,128)} %bitcast.10, f32[1,48]{1,0:T(1,128)} %bitcast.11, ...), custom_call_target="tpu_custom_call" | custom-call | tf_op jit(solution)/shard_map/decays/pallas_call | solution.py:392
  72.4 32.5 %entering_states.1 = (bf16[24,128,128]{2,1,0:T(8,128)(2,1)}, f32[24,512,128]{2,1,0:T(8,128)}, bf16[24,512,256]{2,1,0:T(8,128)(2,1)}, f32[24,3,128,128]{3,2,1,0:T(8,128)}) custom-call(bf16[512,256]{1,0:T(8,128)(2,1)} %get-tuple-element.20.cum_in.cum_ref, f32[24,2,512]{2,1,0:T(2,128)} %get-tuple-element.23.row_in, ...), custom_call_target="tpu_custom_call" | custom-call | tf_op jit(solution)/shard_map/entering_states/pallas_call | solution.py:629
  104.9 25.6 %outputs.1 = (bf16[512,3072]{1,0:T(8,128)(2,1)}, bf16[2,16,80,128]{3,2,1,0:T(8,128)(2,1)}) custom-call(bf16[512,256]{1,0:T(8,128)(2,1)} %get-tuple-element.20.cum_in.cum_ref, bf16[512,128]{1,0:T(8,128)(2,1)} %get-tuple-element.21.c_in.c_ref, bf16[512,128]{1,0:T(8,128)(2,1)} %get-tuple-element.19.b_ref.b_in, s32[32]{0:T(128)} %counts_ref.3, ...), custom_call_target="tpu_custom_call" | custom-call | tf_op jit(solution)/shard_map/outputs/pallas_call | solution.py:420
  130.5 36.1 %reduced_gradient.1 = f32[80,128]{1,0:T(8,128)} custom-call(bf16[2,16,80,128]{3,2,1,0:T(8,128)(2,1)} %get-tuple-element.33.part_ref), custom_call_target="tpu_custom_call" | custom-call | tf_op jit(solution)/shard_map/reduced_gradient/pallas_call | solution.py:706
  166.5 1.4 copy.13
